TPU v7x, 256 devices: a whole 4x4x8 slice. The times are simulated.
256 devices in a mesh: gx: 8 (over x, core), gy: 8 (over z_lo, y), gz: 4 (over z_hi).
Axes of the slice: x: 4, y: 4, z: 8 (z_hi: 4, z_lo: 2; z = z_hi * 2 + z_lo), core: 2. Of those that a mesh axis runs over, the one named last changes fastest.
Arguments:
- grid_inputs: bfloat16 [186, 512, 1024], P(None, 'gx', 'gy'), may hold values from -6 to 6
- embed_w1: bfloat16 [512, 186], replicated, may hold values from -0.4375 to 0.4375
- embed_b1: float32 [512], replicated, may hold values from -3 to 3
- embed_w2: bfloat16 [512, 512], replicated, may hold values from -0.25 to 0.25
- embed_gain: float32 [512], replicated, may hold values from 0.1 to 1.9
- edge_w1: bfloat16 [512, 1536], replicated, may hold values from -0.15625 to 0.15625
- edge_b1: float32 [512], replicated, may hold values from -3 to 3
- edge_w2: bfloat16 [512, 512], replicated, may hold values from -0.25 to 0.25
- message_gain: float32 [512], replicated, may hold values from 0.1 to 1.9
- message_bias: float32 [512], replicated, may hold values from -3 to 3
- mesh_latent: bfloat16 [512, 8, 8, 256], P('gz', 'gx', 'gy'), may hold values from -6 to 6
- edge_latent: bfloat16 [512, 8, 8, 2048], P('gz', 'gx', 'gy'), may hold values from -6 to 6
- senders: int32 [8, 8, 2048], P('gx', 'gy'), may hold values from 0 to 524287, as said below
- receivers: int32 [8, 8, 2048], P('gx', 'gy'), may hold values from 0 to 16383, as said below
- edge_counts: int32 [8, 8], P('gx', 'gy'), may hold values from 1 to 2048, as said below
Outputs:
- mesh_out: bfloat16 [512, 8, 8, 256], P('gz', 'gx', 'gy')
- grid_latent: bfloat16 [512, 512, 1024], P('gz', 'gx', 'gy')
Inputs may be any that keep to these rules, and one draw needn't show every extreme that they name: `senders`: an edge of tile (b, c) has its sender's row within 8 rows of rows b * 64 to (b + 1) * 64 - 1, clipped to the grid, and its column within 8 columns, cyclically, of columns c * 128 to (c + 1) * 128 - 1; this holds in every slot. `receivers`: an edge of tile t is received by a node of that tile, t * 256 to (t + 1) * 256 - 1, in every slot. `edge_counts`: the live edges of a tile are its first slots; some tile holds 2048 live edges.
All inputs are finite; a program needn't handle non-finite values.
Results may differ from a plain program's by a relative error of at most 0.0049.
Values may be sent and summed in bfloat16 or wider, within the bound.
A program may use at most 128 MiB of HBM per device.

v0:
```python
import jax
import jax.numpy as jnp
from jax import lax
from jax.sharding import PartitionSpec as P

HALO = 8
BLOCK = 512


epsilon = 1e-05


def padded_2(value, sides, width):
    for axis, dim in sides:
        size, length = (lax.axis_size(axis), value.shape[dim])
        up = [(i, (i + 1) % size) for i in range(size)]
        down = [(j, i) for i, j in up]
        last = lax.slice_in_dim(value, length - width, length, axis=dim)
        first = lax.slice_in_dim(value, 0, width, axis=dim)
        before = lax.ppermute(last, axis, up)
        after = lax.ppermute(first, axis, down)
        value = jnp.concatenate([before, value, after], axis=dim)
    return value


def sent_to_all(value, axis):
    length = lax.axis_size(axis)
    return lax.all_to_all(
        jnp.broadcast_to(value[None], (length, *value.shape)), axis, 0, 0, tiled=True
    )


def joined_along(pieces, dim):
    pieces = jnp.moveaxis(pieces, 0, dim)
    dims = pieces.shape
    return pieces.reshape(*dims[:dim], dims[dim] * dims[dim + 1], *dims[dim + 2 :])


def gather_directly(value, axis, dim):
    pieces = sent_to_all(value, axis)
    return joined_along(pieces, dim)


def cut_along(value, dim, length):
    before, after = (value.shape[:dim], value.shape[dim + 1 :])
    return jnp.moveaxis(value.reshape(*before, length, -1, *after), dim, 0)


def sum_at_owner(value, axis, dim):
    pieces = cut_along(value, dim, lax.axis_size(axis))
    arrived = lax.all_to_all(pieces, axis, split_axis=0, concat_axis=0, tiled=True)
    return arrived.sum(axis=0)


def normalize(values):
    average = jnp.mean(values, axis=0, keepdims=True)
    centred = values - average
    spread = jnp.mean(centred * centred, axis=0, keepdims=True)
    return centred * lax.rsqrt(spread + epsilon)


def embed_cells(flat_inputs, embed_w1, embed_b1, embed_w2, embed_gain):
    grid_hidden = jax.nn.silu(
        jnp.dot(embed_w1, flat_inputs, preferred_element_type=jnp.float32) + embed_b1[:, None]
    ).astype(jnp.bfloat16)
    grid_pre = jnp.dot(embed_w2, grid_hidden, preferred_element_type=jnp.float32)
    return (normalize(grid_pre) * embed_gain[:, None]).astype(jnp.bfloat16)


def lookup_onehot(mesh_pick, live_mask, node_count):
    node_ids = jnp.arange(node_count, dtype=jnp.int32)
    return ((mesh_pick[:, None] == node_ids[None, :]) & live_mask[:, None]).astype(jnp.bfloat16)


def first_layer(weight_rows, bias_rows, edge_block, grid_cols, mesh_cols, latent):
    first_pre = jnp.dot(weight_rows[:, :latent], edge_block, preferred_element_type=jnp.float32)
    first_pre = first_pre + jnp.dot(
        weight_rows[:, latent : 2 * latent], grid_cols, preferred_element_type=jnp.float32
    )
    first_pre = first_pre + jnp.dot(
        weight_rows[:, 2 * latent :], mesh_cols, preferred_element_type=jnp.float32
    )
    return jax.nn.silu(first_pre + bias_rows[:, None]).astype(jnp.bfloat16)


def on_device(
    grid_inputs,
    embed_w1,
    embed_b1,
    embed_w2,
    embed_gain,
    edge_w1,
    edge_b1,
    edge_w2,
    message_gain,
    message_bias,
    mesh_latent,
    edge_latent,
    senders,
    receivers,
    edge_counts,
):
    latent = embed_w2.shape[0]
    channel_count = grid_inputs.shape[0]
    shard_rows = mesh_latent.shape[0]
    lat_rows = grid_inputs.shape[1]
    lon_cols = grid_inputs.shape[2]
    cell_count = lat_rows * lon_cols
    node_count = mesh_latent.shape[3]
    slot_count = edge_latent.shape[3]
    layer_size = lax.axis_size("gz")
    layer_index = lax.axis_index("gz")
    band_index = lax.axis_index("gx")
    sector = lax.axis_index("gy")
    lon_total = lon_cols * lax.axis_size("gy")
    live_count = edge_counts[0, 0]
    padded_cells = (lat_rows + 2 * HALO) * (lon_cols + 2 * HALO)
    row_start = layer_index * shard_rows
    own_latent = embed_cells(
        grid_inputs.reshape(channel_count, cell_count), embed_w1, embed_b1, embed_w2, embed_gain
    ).reshape(latent, lat_rows, lon_cols)
    padded = padded_2(own_latent, (("gx", 1), ("gy", 2)), HALO)
    pad_flat = padded.reshape(latent, padded_cells)
    grid_out = lax.dynamic_slice_in_dim(own_latent, row_start, shard_rows, 0)
    send_all = senders[0, 0]
    lat_local = send_all // lon_total - band_index * lat_rows + HALO
    lon_local = (send_all % lon_total - sector * lon_cols + HALO + lon_total) % lon_total
    grid_index = lat_local * (lon_cols + 2 * HALO) + lon_local
    tile_index = band_index * lax.axis_size("gy") + sector
    near_index = receivers[0, 0] - tile_index * node_count
    slot_ids = jnp.arange(slot_count, dtype=jnp.int32)
    live_all = slot_ids < live_count
    node_ids = jnp.arange(node_count, dtype=jnp.int32)
    degree = jnp.sum(
        ((near_index[:, None] == node_ids[None, :]) & live_all[:, None]).astype(jnp.int32), axis=0
    )
    mesh_own = mesh_latent[:, 0, 0, :]
    edge_own = edge_latent[:, 0, 0, :]
    lead_size, tail_size = (1, slot_count // layer_size)
    arranged = edge_own.reshape(shard_rows, lead_size, layer_size, tail_size)
    assigned = lax.all_to_all(arranged, "gz", split_axis=2, concat_axis=0, tiled=True).reshape(
        latent, lead_size * tail_size
    )
    mesh_full = gather_directly(mesh_own, "gz", 0)
    lead_ids = jnp.arange(lead_size, dtype=jnp.int32)[:, None]
    tail_ids = jnp.arange(tail_size, dtype=jnp.int32)[None, :]
    my_slots = ((lead_ids * layer_size + layer_index) * tail_size + tail_ids).reshape(
        lead_size * tail_size
    )
    my_grid = jnp.take(grid_index, my_slots)
    my_near = jnp.take(near_index, my_slots)
    block_starts = my_slots.reshape(-1, BLOCK)[:, 0]
    live_blocks = jnp.sum((block_starts < live_count).astype(jnp.int32))

    def advance_full(block_index, totals):
        live_mask = my_slots < live_count
        onehot = lookup_onehot(my_near, live_mask, node_count)
        grid_cols = jnp.take(pad_flat, my_grid, axis=1)
        mesh_cols = lax.dot_general(
            mesh_full, onehot, (((1,), (1,)), ((), ())), preferred_element_type=jnp.float32
        ).astype(jnp.bfloat16)
        hidden = first_layer(edge_w1, edge_b1, assigned, grid_cols, mesh_cols, latent)
        second = jnp.dot(edge_w2, hidden, preferred_element_type=jnp.float32)
        message = (
            assigned.astype(jnp.float32)
            + normalize(second) * message_gain[:, None]
            + message_bias[:, None]
        ).astype(jnp.bfloat16)
        return totals + jnp.dot(message, onehot, preferred_element_type=jnp.float32)

    partial_totals = lax.fori_loop(
        0, live_blocks, advance_full, jnp.zeros((latent, node_count), jnp.float32)
    )
    totals_own = sum_at_owner(partial_totals, "gz", 0)
    scale = jnp.maximum(degree, 1).astype(jnp.float32)
    result = mesh_own.astype(jnp.float32) + totals_own / scale[None, :]
    return (result.astype(jnp.bfloat16).reshape(shard_rows, 1, 1, node_count), grid_out)


def solution(mesh):
    return jax.shard_map(
        on_device,
        mesh=mesh,
        in_specs=(
            P(None, "gx", "gy"),
            P(),
            P(),
            P(),
            P(),
            P(),
            P(),
            P(),
            P(),
            P(),
            P("gz", "gx", "gy", None),
            P("gz", "gx", "gy", None),
            P("gx", "gy", None),
            P("gx", "gy", None),
            P("gx", "gy"),
        ),
        out_specs=(P("gz", "gx", "gy", None), P("gz", "gx", "gy")),
        check_vma=False,
    )
```

profile of v0, /device:TPU:32, one launch (start us, length us, event | category | flops | bytes accessed | tf_op | source)
XLA Modules:
  0.0 136.0 jit_solution(17378626972182538780)
XLA Ops:
  0.6 0.0 copy-start
  0.7 2.6 %pad.17 = bf16[192,64,128]{2,1,0:T(8,128)(2,1)S(1)} pad(bf16[186,64,128]{2,1,0:T(8,128)(2,1)} %param.19, bf16[]{:T(256)} %constant.182), padding=0_6x0_0x0_0 | pad | bytes 6193154
  3.3 4.5 %copy.41 = bf16[24,8,64,128]{3,1,2,0:T(8,128)(2,1)} copy(bf16[24,8,64,128]{3,2,1,0:T(8,128)(2,1)S(1)} %bitcast.62) | data formatting | bytes 6291456
  7.8 0.0 copy-done.10
  7.8 14.6 %fusion.45 = (f32[8192]{0:T(1024)S(1)}, f32[8192,512]{1,0:T(8,128)}) fusion(bf16[512,512]{1,0:T(8,128)(2,1)S(1)} %copy-done, bf16[512,186]{0,1:T(8,128)(2,1)S(1)} %copy-done.10, bf16[186,8192]{1,0:T(8,128)(2,1)} %bitcast.63, f32[512]{0:T(512)S(1)} %copy-done.11), kind=kOutput, calls=%fused_computation.84 | convolution fusion | flops 5884600320 | bytes 20574208 | tf_op jit(solution)/shard_map/dot_general | solution.py:66
  22.4 8.6 %multiply_reduce_fusion = f32[8192]{0:T(1024)S(1)} fusion(f32[8192,512]{1,0:T(8,128)} %get-tuple-element.407, f32[8192]{0:T(1024)S(1)} %broadcast_multiply_fusion), kind=kLoop, calls=%fused_computation.4 | loop fusion | flops 12574720 | bytes 16842752 | tf_op jit(solution)/shard_map/reduce_sum | solution.py:58
  31.0 2.0 %copy-done.3 = f32[8192,512]{1,0:T(8,128)S(1)} copy-done((f32[8192,512]{1,0:T(8,128)S(1)}, f32[8192,512]{1,0:T(8,128)}, u32[]{:S(2)}) %copy-start.3) | copy-done | bytes 16777240
  33.1 4.5 %multiply_convert_fusion = bf16[8192,512]{1,0:T(8,128)(2,1)S(1)} fusion(f32[8192,512]{1,0:T(8,128)S(1)} %copy-done.3, f32[512]{0:T(512)S(1)} %copy-done.9, f32[8192]{0:T(1024)S(1)} %add_rsqrt_fusion, f32[8192]{0:T(1024)S(1)} %broadcast_multiply_fusion), kind=kLoop, calls=%fused_computation.3 | loop fusion | flops 16777216 | bytes 25233408 | tf_op jit(solution)/shard_map/convert_element_type | solution.py:67
  37.6 0.0 copy-start.6
  37.6 3.2 %copy-done.2 = bf16[8192,512]{1,0:T(8,128)(2,1)} copy-done((bf16[8192,512]{1,0:T(8,128)(2,1)}, bf16[8192,512]{1,0:T(8,128)(2,1)S(1)}, u32[]{:S(2)}) %copy-start.2) | copy-done | bytes 8388632
  40.8 1.5 %fusion.44 = (bf16[512,8,128]{0,2,1:T(8,128)(2,1)}, bf16[512,8,128]{0,2,1:T(8,128)(2,1)}) fusion(bf16[512,64,128]{0,2,1:T(8,128)(2,1)S(1)} %bitcast.57), kind=kLoop, calls=%fused_computation.83 | loop fusion | bytes 4194304 | tf_op jit(solution)/shard_map/slice | solution.py:18
  42.3 0.0 collective-permute-start
  42.3 3.0 %collective-permute-start.1 = (bf16[512,8,128]{0,2,1:T(8,128)(2,1)}, bf16[512,8,128]{0,2,1:T(8,128)(2,1)S(1)}, u32[]{:S(2)}, u32[]{:S(2)}) collective-permute-start(bf16[512,8,128]{0,2,1:T(8,128)(2,1)} %get-tuple-element.405), channel_id=1, source_target_pairs={{32,0},{64,32},{96,64},{128,96},{160,128},{192,160},{224,192},{0,2... | collective-permute-start | bytes 3145736 | tf_op jit(solution)/shard_map/ppermute | solution.py:21
  45.2 0.3 copy.33
  45.5 1.0 copy.34
  46.5 7.6 %all-to-all-start = ((bf16[128,1,4,512]{3,0,1,2:T(8,128)(2,1)}), bf16[128,1,4,512]{3,0,1,2:T(8,128)(2,1)S(1)}, u32[]{:S(2)}, u32[]{:S(2)}) async-start(bf16[128,1,4,512]{3,0,1,2:T(8,128)(2,1)} %copy.34), calls=%async_computation | async-start | bytes 1048576 | tf_op jit(solution)/shard_map/all_to_all | solution.py:141
  54.8 3.1 %gather_fusion.1 = s32[512]{0:T(512)S(1)} fusion(s32[2048]{0:T(1024)S(1)} %fusion.35, s32[1024]{0:T(1024)S(1)} %pad_clamp_fusion.1), kind=kCustom, calls=%fused_computation.clone | custom fusion | bytes 6144 | tf_op jit(solution)/shard_map/jit(_take)/gather | solution.py:150
  58.0 0.0 collective-permute-done
  58.0 0.0 collective-permute-done.1
  58.0 2.4 %pad_maximum_fusion.3 = (bf16[512,80,8]{0,2,1:T(8,128)(2,1)}, bf16[512,80,8]{0,2,1:T(8,128)(2,1)}) fusion(bf16[512,8,128]{0,2,1:T(8,128)(2,1)S(1)} %collective-permute-done.1, bf16[512,64,128]{0,2,1:T(8,128)(2,1)} %bitcast.58, bf16[512,8,128]{0,2,1:T(8,128)(2,1)S(1)} %collective-permute-done), kind=kLoop, calls=%fused_computation.24 | loop fusion | flops 3932160 | bytes 11796480 | tf_op jit(solution)/shard_map/slice | solution.py:18
  60.4 1.6 %collective-permute-start.2 = (bf16[512,80,8]{0,2,1:T(8,128)(2,1)}, bf16[512,80,8]{0,2,1:T(8,128)(2,1)}, u32[]{:S(2)}, u32[]{:S(2)}) collective-permute-start(bf16[512,80,8]{0,2,1:T(8,128)(2,1)} %get-tuple-element.402), channel_id=1, source_target_pairs={{0,4},{4,8},{8,12},{12,16},{16,20},{20,24},{24,28},{28,0},{1,5},{5... | collective-permute-start | bytes 1966088 | tf_op jit(solution)/shard_map/ppermute | solution.py:20
  62.0 2.6 %collective-permute-start.3 = (bf16[512,80,8]{0,2,1:T(8,128)(2,1)}, bf16[512,80,8]{0,2,1:T(8,128)(2,1)}, u32[]{:S(2)}, u32[]{:S(2)}) collective-permute-start(bf16[512,80,8]{0,2,1:T(8,128)(2,1)} %get-tuple-element.403), channel_id=1, source_target_pairs={{4,0},{8,4},{12,8},{16,12},{20,16},{24,20},{28,24},{0,28},{5,1},{9... | collective-permute-start | bytes 1966088 | tf_op jit(solution)/shard_map/ppermute | solution.py:21
  64.6 3.1 %gather_fusion.2 = s32[512]{0:T(512)S(1)} fusion(s32[2048]{0:T(1024)S(1)} %bitcast.55, s32[1024]{0:T(1024)S(1)} %pad_clamp_fusion.1), kind=kCustom, calls=%fused_computation.1.clone | custom fusion | bytes 6144 | tf_op jit(solution)/shard_map/jit(_take)/gather | solution.py:151
  67.7 1.7 %all-to-all-done = bf16[128,1,4,512]{3,0,1,2:T(8,128)(2,1)S(1)} async-done(((bf16[128,1,4,512]{3,0,1,2:T(8,128)(2,1)}), bf16[128,1,4,512]{3,0,1,2:T(8,128)(2,1)S(1)}, u32[]{:S(2)}, u32[]{:S(2)}) %all-to-all-start) | async-done | bytes 524320 | tf_op jit(solution)/shard_map/all_to_all | solution.py:141
  69.4 0.7 broadcast_in_dim.53
  70.2 5.8 %all-to-all-start.1 = ((bf16[4,128,256]{2,1,0:T(8,128)(2,1)}), bf16[4,128,256]{2,1,0:T(8,128)(2,1)S(1)}, u32[]{:S(2)}, u32[]{:S(2)}) async-start(bf16[4,128,256]{2,1,0:T(8,128)(2,1)} %broadcast_in_dim.53), calls=%async_computation.1 | async-start | bytes 524288 | tf_op jit(solution)/shard_map/all_to_all | solution.py:28
  76.0 2.4 %fusion.16 = f32[512,512]{1,0:T(8,128)} fusion(bf16[512,512]{1,0:T(8,128)(2,1)S(1)} %bitcast.65, bf16[512,1536]{1,0:T(8,128)(2,1)} %param.24), kind=kOutput, calls=%fused_computation.34 | convolution fusion | flops 268435456 | bytes 2097152 | tf_op jit(solution)/shard_map/while/body/dot_general | solution.py:76
  78.4 6.2 %collective-permute-done.2 = bf16[512,80,8]{0,2,1:T(8,128)(2,1)} collective-permute-done((bf16[512,80,8]{0,2,1:T(8,128)(2,1)}, bf16[512,80,8]{0,2,1:T(8,128)(2,1)}, u32[]{:S(2)}, u32[]{:S(2)}) %collective-permute-start.2) | collective-permute-done | bytes 655392 | tf_op jit(solution)/shard_map/ppermute | solution.py:20
  84.6 0.0 collective-permute-done.3
  84.6 12.1 %pad_maximum_fusion = bf16[512,80,144]{0,2,1:T(8,128)(2,1)} fusion(bf16[512,80,8]{0,2,1:T(8,128)(2,1)} %collective-permute-done.3, bf16[512,8,128]{0,2,1:T(8,128)(2,1)S(1)} %collective-permute-done.1, bf16[512,64,128]{0,2,1:T(8,128)(2,1)} %bitcast.59, bf16[512,8,128]{0,2,1:T(8,128)(2,1)S(1)} %collective-permute-done, ...), kind=kLoop, calls=%fused_computation.6 | loop fusion | flops 58982400 | bytes 23592960 | tf_op jit(solution)/shard_map/concatenate | solution.py:22
  96.7 7.9 %gather_fusion = bf16[512,512]{1,0:T(8,128)(2,1)S(1)} fusion(bf16[512,11520]{0,1:T(8,128)(2,1)} %bitcast.61, s32[1024]{0:T(1024)S(1)} %pad_clamp_fusion), kind=kCustom, calls=%fused_computation.2 | custom fusion | bytes 1050624 | tf_op jit(solution)/shard_map/while/body/jit(_take)/gather | solution.py:158
  104.7 1.9 %fusion.3 = f32[512,512]{1,0:T(8,128)S(1)} fusion(f32[512,512]{1,0:T(8,128)} %fusion.16, bf16[512,512]{1,0:T(8,128)(2,1)S(1)} %gather_fusion, bf16[512,1536]{1,0:T(8,128)(2,1)} %param.24, pred[512]{0:T(512)(128)(4,1)S(1)} %get-tuple-element.400), kind=kOutput, calls=%fused_computation.14 | convolution fusion | flops 268959744 | bytes 3146240 | tf_op jit(solution)/shard_map/while/body/dot_general | solution.py:77
  106.6 0.0 all-to-all-done.1
  106.6 0.0 copy-start.1
  106.6 1.9 %multiply_convert_fusion.2 = bf16[512,512]{1,0:T(8,128)(2,1)S(1)} fusion(f32[512,512]{1,0:T(8,128)S(1)} %fusion.3, bf16[512,256]{1,0:T(8,128)(2,1)S(1)} %bitcast.67, f32[512]{0:T(512)S(1)} %copy-done.12, bf16[512,1536]{1,0:T(8,128)(2,1)} %param.24, s32[512]{0:T(512)S(1)} %broadcast_select_fusion, pred[512]{0:T(512)(128)(4,1)S(1)} %fusion.41), kind=kOutput, calls=%fused_computation.20 | convolution fusion | flops 405012480 | bytes 2363904 | tf_op jit(solution)/shard_map/while/body/dot_general | solution.py:80
  108.6 0.4 fusion.46
  109.1 0.2 multiply_reduce_fusion.1
  109.3 0.0 copy-done.14
  109.3 0.6 fusion.7
  109.8 0.8 broadcast_in_dim.28
  110.7 1.9 %while.17 = (s32[]{:T(128)}, f32[512,256]{1,0:T(8,128)}, s32[]{:T(128)}, f32[512,256]{1,0:T(8,128)S(1)}, s32[]{:T(128)}) while((s32[]{:T(128)}, f32[512,256]{1,0:T(8,128)}, s32[]{:T(128)}, f32[512,256]{1,0:T(8,128)S(1)}, s32[]{:T(128)}) %tuple.53), condition=%wide.region_5.7_spmd, body=%wide.region_4.6_spmd.sunk | while | flops 131074 | bytes 1572925 | solution.py:171
  110.7 1.9 %add.374 = f32[512,256]{1,0:T(8,128)} add(f32[512,256]{1,0:T(8,128)} %get-tuple-element.442, f32[512,256]{1,0:T(8,128)S(1)} %get-tuple-element.449) | non-fusion elementwise | flops 131072 | bytes 1572864 | tf_op jit(solution)/shard_map/while/body/add | solution.py:169
  112.6 5.8 %all-to-all-start.2 = ((f32[4,128,256]{2,1,0:T(8,128)}), f32[4,128,256]{2,1,0:T(8,128)S(1)}, u32[]{:S(2)}, u32[]{:S(2)}) async-start(f32[4,128,256]{2,1,0:T(8,128)} %bitcast.19), calls=%async_computation.2 | async-start | bytes 1048576 | tf_op jit(solution)/shard_map/all_to_all | solution.py:51
  118.3 1.7 %constant_dynamic-slice_fusion = bf16[128,64,128]{0,2,1:T(8,128)(2,1)S(1)} fusion(bf16[512,64,128]{0,2,1:T(8,128)(2,1)} %bitcast.60, s32[]{:T(128)S(6)} %select_n.56), kind=kLoop, calls=%fused_computation.80 | loop fusion | bytes 4194308 | tf_op jit(solution)/shard_map/dynamic_slice | solution.py:124
  120.1 2.8 %copy.40 = bf16[128,64,128]{2,1,0:T(8,128)(2,1)} copy(bf16[128,64,128]{0,2,1:T(8,128)(2,1)S(1)} %constant_dynamic-slice_fusion) | data formatting | bytes 4194304
  122.8 1.4 %convert_reduce_fusion = s32[256]{0:T(256)S(1)} fusion(s32[2048]{0:T(1024)S(1)} %bitcast.56, pred[2048]{0:T(1024)(128)(4,1)S(1)} %iota_compare_fusion.2), kind=kLoop, calls=%fused_computation.7 | loop fusion | flops 2096896 | bytes 11264 | tf_op jit(solution)/shard_map/reduce_sum | solution.py:134
  124.2 11.0 %all-to-all-done.2 = f32[4,128,256]{2,1,0:T(8,128)S(1)} async-done(((f32[4,128,256]{2,1,0:T(8,128)}), f32[4,128,256]{2,1,0:T(8,128)S(1)}, u32[]{:S(2)}, u32[]{:S(2)}) %all-to-all-start.2) | async-done | bytes 524320 | tf_op jit(solution)/shard_map/all_to_all | solution.py:51
  135.3 0.7 fusion.31
  (39 shorter events, 0.2 us)
Async XLA Ops:
  0.6 7.2 %copy-start = (bf16[512,512]{1,0:T(8,128)(2,1)S(1)}, bf16[512,512]{1,0:T(8,128)(2,1)}, u32[]{:S(2)}) copy-start(bf16[512,512]{1,0:T(8,128)(2,1)} %param.22) | copy-start | bytes 1572868
  0.6 7.1 %copy-start.10 = (bf16[512,186]{0,1:T(8,128)(2,1)S(1)}, bf16[512,186]{0,1:T(8,128)(2,1)}, u32[]{:S(2)}) copy-start(bf16[512,186]{0,1:T(8,128)(2,1)} %param.20) | copy-start | bytes 571396
  0.7 7.1 %copy-start.11 = (f32[512]{0:T(512)S(1)}, f32[512]{0:T(512)}, u32[]{:S(2)}) copy-start(f32[512]{0:T(512)} %param.21) | copy-start | bytes 6148
  22.4 10.7 %copy-start.3 = (f32[8192,512]{1,0:T(8,128)S(1)}, f32[8192,512]{1,0:T(8,128)}, u32[]{:S(2)}) copy-start(f32[8192,512]{1,0:T(8,128)} %get-tuple-element.407) | copy-start | bytes 50331652
  22.4 10.7 %copy-start.9 = (f32[512]{0:T(512)S(1)}, f32[512]{0:T(512)}, u32[]{:S(2)}) copy-start(f32[512]{0:T(512)} %param.23) | copy-start | bytes 6148
  33.0 12.2 %copy-start.5 = (bf16[128,1,1,2048]{3,0,2,1:T(8,128)(2,1)S(1)}, bf16[128,1,1,2048]{3,0,2,1:T(8,128)(2,1)}, u32[]{:S(2)}) copy-start(bf16[128,1,1,2048]{3,0,2,1:T(8,128)(2,1)} %param.30) | copy-start | bytes 1572868
  33.0 21.7 %copy-start.7 = (s32[1,1,2048]{2,1,0:T(1,128)S(1)}, s32[1,1,2048]{2,1,0:T(1,128)}, u32[]{:S(2)}) copy-start(s32[1,1,2048]{2,1,0:T(1,128)} %param.31) | copy-start | bytes 24580
  33.0 24.9 %copy-start.8 = (s32[1,1,2048]{2,1,0:T(1,128)S(1)}, s32[1,1,2048]{2,1,0:T(1,128)}, u32[]{:S(2)}) copy-start(s32[1,1,2048]{2,1,0:T(1,128)} %param.32) | copy-start | bytes 24580
  37.5 3.2 %copy-start.2 = (bf16[8192,512]{1,0:T(8,128)(2,1)}, bf16[8192,512]{1,0:T(8,128)(2,1)S(1)}, u32[]{:S(2)}) copy-start(bf16[8192,512]{1,0:T(8,128)(2,1)S(1)} %multiply_convert_fusion) | copy-start | bytes 25165828
  37.6 31.9 %copy-start.6 = (bf16[128,1,1,256]{3,0,2,1:T(8,128)(2,1)S(1)}, bf16[128,1,1,256]{3,0,2,1:T(8,128)(2,1)}, u32[]{:S(2)}) copy-start(bf16[128,1,1,256]{3,0,2,1:T(8,128)(2,1)} %param.29) | copy-start | bytes 196612
  42.3 15.7 %collective-permute-start = (bf16[512,8,128]{0,2,1:T(8,128)(2,1)}, bf16[512,8,128]{0,2,1:T(8,128)(2,1)S(1)}, u32[]{:S(2)}, u32[]{:S(2)}) collective-permute-start(bf16[512,8,128]{0,2,1:T(8,128)(2,1)} %get-tuple-element.404), channel_id=1, source_target_pairs={{0,32},{32,64},{64,96},{96,128},{128,160},{160,192},{192,224},{224... | collective-permute-start | bytes 3145736 | tf_op jit(solution)/shard_map/ppermute | solution.py:20
  42.3 15.7 %collective-permute-start.1 = (bf16[512,8,128]{0,2,1:T(8,128)(2,1)}, bf16[512,8,128]{0,2,1:T(8,128)(2,1)S(1)}, u32[]{:S(2)}, u32[]{:S(2)}) collective-permute-start(bf16[512,8,128]{0,2,1:T(8,128)(2,1)} %get-tuple-element.405), channel_id=1, source_target_pairs={{32,0},{64,32},{96,64},{128,96},{160,128},{192,160},{224,192},{0,2... | collective-permute-start | bytes 3145736 | tf_op jit(solution)/shard_map/ppermute | solution.py:21
  46.5 22.9 %all-to-all-start = ((bf16[128,1,4,512]{3,0,1,2:T(8,128)(2,1)}), bf16[128,1,4,512]{3,0,1,2:T(8,128)(2,1)S(1)}, u32[]{:S(2)}, u32[]{:S(2)}) async-start(bf16[128,1,4,512]{3,0,1,2:T(8,128)(2,1)} %copy.34), calls=%async_computation | async-start | bytes 1048576 | tf_op jit(solution)/shard_map/all_to_all | solution.py:141
  60.4 24.2 %collective-permute-start.2 = (bf16[512,80,8]{0,2,1:T(8,128)(2,1)}, bf16[512,80,8]{0,2,1:T(8,128)(2,1)}, u32[]{:S(2)}, u32[]{:S(2)}) collective-permute-start(bf16[512,80,8]{0,2,1:T(8,128)(2,1)} %get-tuple-element.402), channel_id=1, source_target_pairs={{0,4},{4,8},{8,12},{12,16},{16,20},{20,24},{24,28},{28,0},{1,5},{5... | collective-permute-start | bytes 1966088 | tf_op jit(solution)/shard_map/ppermute | solution.py:20
  62.0 22.6 %collective-permute-start.3 = (bf16[512,80,8]{0,2,1:T(8,128)(2,1)}, bf16[512,80,8]{0,2,1:T(8,128)(2,1)}, u32[]{:S(2)}, u32[]{:S(2)}) collective-permute-start(bf16[512,80,8]{0,2,1:T(8,128)(2,1)} %get-tuple-element.403), channel_id=1, source_target_pairs={{4,0},{8,4},{12,8},{16,12},{20,16},{24,20},{28,24},{0,28},{5,1},{9... | collective-permute-start | bytes 1966088 | tf_op jit(solution)/shard_map/ppermute | solution.py:21
  70.2 36.5 %all-to-all-start.1 = ((bf16[4,128,256]{2,1,0:T(8,128)(2,1)}), bf16[4,128,256]{2,1,0:T(8,128)(2,1)S(1)}, u32[]{:S(2)}, u32[]{:S(2)}) async-start(bf16[4,128,256]{2,1,0:T(8,128)(2,1)} %broadcast_in_dim.53), calls=%async_computation.1 | async-start | bytes 524288 | tf_op jit(solution)/shard_map/all_to_all | solution.py:28
  78.4 28.2 %copy-start.12 = (f32[512]{0:T(512)S(1)}, f32[512]{0:T(512)}, u32[]{:S(2)}) copy-start(f32[512]{0:T(512)} %param.25) | copy-start | bytes 6148
  96.7 11.9 %copy-start.4 = (bf16[512,512]{1,0:T(8,128)(2,1)S(1)}, bf16[512,512]{1,0:T(8,128)(2,1)}, u32[]{:S(2)}) copy-start(bf16[512,512]{1,0:T(8,128)(2,1)} %param.26) | copy-start | bytes 1572868
  96.7 12.5 %copy-start.13 = (f32[512]{0:T(512)S(1)}, f32[512]{0:T(512)}, u32[]{:S(2)}) copy-start(f32[512]{0:T(512)} %param.28) | copy-start | bytes 6148
  96.7 12.5 %copy-start.14 = (f32[512]{0:T(512)S(1)}, f32[512]{0:T(512)}, u32[]{:S(2)}) copy-start(f32[512]{0:T(512)} %param.27) | copy-start | bytes 6148
  106.6 29.3 %copy-start.1 = (bf16[512,512]{1,0:T(8,128)(2,1)S(1)}, bf16[512,512]{1,0:T(8,128)(2,1)}, u32[]{:S(2)}) copy-start(bf16[512,512]{1,0:T(8,128)(2,1)} %param.22) | copy-start | bytes 1572868
  112.6 22.7 %all-to-all-start.2 = ((f32[4,128,256]{2,1,0:T(8,128)}), f32[4,128,256]{2,1,0:T(8,128)S(1)}, u32[]{:S(2)}, u32[]{:S(2)}) async-start(f32[4,128,256]{2,1,0:T(8,128)} %bitcast.19), calls=%async_computation.2 | async-start | bytes 1048576 | tf_op jit(solution)/shard_map/all_to_all | solution.py:51
where the time goes:
time: 137 us; the launch traced here: 136 us
  local copies, waits for them, and re-layouts  35.5 us (26%)
  other arithmetic  31.9 us (23%)
  starting transfers between devices  26.2 us (19%)
  matrix products  21.9 us (16%)
  waiting for transfers between devices  18.9 us (14%)
  between operations  1.59 us (1%)
    unnamed x34, local copies, waits for them, and re-layouts  15.5 us
    dot_general x1, matrix products, embed_cells(): jnp.dot(embed_w2, grid_hidden, preferred_element_type=jnp.float32)  14.6 us
    concatenate x1, other arithmetic, padded_2(): value = jnp.concatenate([before, value, after], axis=dim)  12.1 us
    all_to_all x1, waiting for transfers between devices, sum_at_owner(): lax.all_to_all(pieces, axis, split_axis=0, concat_axis=0, tiled=True)  11 us
    reduce_sum x2, other arithmetic, normalize(): spread = jnp.mean(centred * centred, axis=0, keepdims=True)  8.8 us
    gather x1, local copies, waits for them, and re-layouts, advance_full(): grid_cols = jnp.take(pad_flat, my_grid, axis=1)  7.91 us
    all_to_all x1, starting transfers between devices, on_device(): lax.all_to_all(arranged, 'gz', split_axis=2, concat_axis=0, tiled=True)  7.56 us
    ppermute x2, waiting for transfers between devices, padded_2(): before = lax.ppermute(last, axis, up)  6.18 us
  transfers between devices with their start and end apart: 7, of which 3 were waited for; matrix products, arithmetic and copies ran while one was open for 30% of the time, Pallas kernels for 0%

commit v1 on v0

v1 whole, which is shorter than its diff:
```python
import functools

import jax
import jax.numpy as jnp
from jax import lax
from jax.experimental import pallas as pl
from jax.experimental.pallas import tpu as pltpu
from jax.sharding import PartitionSpec as P

HALO = 8
EPS = 1e-05
F32 = jnp.float32
BF16 = jnp.bfloat16
TILE = 512
ROWS = 16
KPAD = 192


def dot(a, b):
    return jnp.dot(a, b, preferred_element_type=F32)


def dot_nt(a, b):
    return lax.dot_general(a, b, (((1,), (1,)), ((), ())), preferred_element_type=F32)


def half_silu(h):
    return (h + h * jnp.tanh(h)).astype(BF16)


def centred(values):
    average = jnp.mean(values, axis=0, keepdims=True)
    c = values - average
    spread = jnp.mean(c * c, axis=0, keepdims=True)
    return c, lax.rsqrt(spread + EPS)


def wide(column, times):
    return jnp.concatenate([column] * times, axis=1)


def kernel(
    sizes,
    x_hbm, w1t_hbm, w2_hbm, ew1_hbm, ew2_hbm,
    b1_ref, gain_ref, eb1_ref, mgain_ref, mbias_ref,
    mesh_hbm, edge_hbm, send_ref, recv_ref, count_ref,
    out_mesh, out_grid,
    x_v, w1t_v, w2_v, w2r_v, ew1_v, ew2_v, e_own, mesh_own, edges, mesh_full,
    north, south, west, east, corner,
    xf, xc, xh, w1f, w1p, cols, sel, strip, gath, outf, ob, tot, tb, tr,
    local, wsend, wrecv, bar_unused,
):
    gx_n, gy_n, gz_n = sizes
    channels, lat_rows, lon_cols = x_hbm.shape
    latent = w2_v.shape[0]
    share = latent // gz_n
    slots = edge_hbm.shape[1]
    mine = slots // gz_n
    nodes = mesh_hbm.shape[1]
    blocks = lat_rows // ROWS
    gx, gy, gz = lax.axis_index("gx"), lax.axis_index("gy"), lax.axis_index("gz")
    up, down = lax.rem(gx + gx_n - 1, gx_n), lax.rem(gx + 1, gx_n)
    left, right = lax.rem(gy + gy_n - 1, gy_n), lax.rem(gy + 1, gy_n)
    peers = [lax.rem(gz + d, gz_n) for d in range(1, gz_n)]

    places = [{"gz": p} for p in peers]
    places += [{"gx": up}, {"gx": down}, {"gy": left}, {"gy": right}]
    places += [{"gx": a, "gy": b} for a in (up, down) for b in (left, right)]
    barrier = pltpu.get_barrier_semaphore()
    for place in places:
        pl.semaphore_signal(barrier, inc=1, device_id=place, device_id_type=pl.DeviceIdType.MESH)

    def own(index, size=share):
        return pl.ds(pl.multiple_of(index * size, 128), size)

    copies = []

    def bring(src, dst):
        copy = pltpu.make_async_copy(src, dst, local.at[len(copies)])
        copy.start()
        copies.append(copy)
        return copy

    x_in = [bring(x_hbm.at[:, pl.ds(i * ROWS, ROWS), :], x_v.at[i]) for i in range(blocks)]
    w1_in = bring(w1t_hbm, w1t_v)
    w2r_in = [
        bring(w2_hbm.at[own(lax.rem(gz + j, gz_n)), :], w2r_v.at[pl.ds(j * share, share), :])
        for j in range(gz_n)
    ]
    w2_in = bring(w2_hbm, w2_v)
    edge_in = bring(edge_hbm.at[:, own(gz, mine)], edges.at[own(gz), :])
    mesh_in = bring(mesh_hbm, mesh_full.at[own(gz), :])
    mown_in = bring(mesh_hbm, mesh_own)
    eown_in = bring(edge_hbm, e_own)
    ew1_in = bring(ew1_hbm, ew1_v)
    ew2_in = bring(ew2_hbm, ew2_v)

    w1_in.wait()
    w1f[...] = jnp.zeros_like(w1f)
    w1f[0:channels, :] = w1t_v[...].astype(F32) * 0.5
    half_b = b1_ref[...] * 0.5
    for k in range(3):
        piece = half_b.astype(BF16).astype(F32)
        w1f[channels + k : channels + k + 1, :] = piece
        half_b = half_b - piece
    w1p[...] = jnp.transpose(w1f[...])[:, :KPAD].astype(BF16)
    for k, ref in enumerate((gain_ref, eb1_ref, mgain_ref, mbias_ref)):
        cols[k] = jnp.transpose(jnp.broadcast_to(ref[...], (128, latent)))
    pad_rows = lax.broadcasted_iota(jnp.int32, ((KPAD - channels) * ROWS, 128), 0)
    pad_values = jnp.where(pad_rows < 3 * ROWS, 1.0, 0.0).astype(F32)
    xf[pl.ds(channels * ROWS, (KPAD - channels) * ROWS), :] = pad_values

    pl.semaphore_wait(barrier, len(places))
    sent = []

    def send(src, dst, place):
        n = len(sent)
        copy = pltpu.make_async_remote_copy(
            src_ref=src, dst_ref=dst, send_sem=wsend.at[n], recv_sem=wrecv.at[n],
            device_id=place, device_id_type=pl.DeviceIdType.MESH,
        )
        copy.start()
        sent.append(copy)
        return copy

    order = [1, 0, 2] if gz_n == 4 else list(range(gz_n - 1))
    mesh_moves = [send(mesh_hbm, mesh_full.at[own(gz), :], {"gz": peers[d]}) for d in order]
    edge_moves = [
        send(edge_hbm.at[:, own(peers[d], mine)], edges.at[own(gz), :], {"gz": peers[d]})
        for d in order
    ]
    row_moves = [
        send(x_hbm.at[:, pl.ds(0, HALO), :], south, {"gx": up}),
        send(x_hbm.at[:, pl.ds(lat_rows - HALO, HALO), :], north, {"gx": down}),
    ]

    sub = TILE // lon_cols
    for q in range(ROWS // sub):
        k = lax.broadcasted_iota(jnp.int32, (TILE, 256), 0)
        j = lax.broadcasted_iota(jnp.int32, (TILE, 256), 1)
        side, jj = j >> 7, j & 127
        want = ((jj >> 3) - q * sub) * lon_cols + side * (lon_cols - HALO) + (jj & 7)
        sel[q] = jnp.where(k == want, 1.0, 0.0).astype(BF16)

    per = ROWS // sub

    def relayout(i, carry):
        xf[pl.ds(0, channels * ROWS), :] = x_v[i].astype(F32).reshape(channels * ROWS, lon_cols)
        for l in range(ROWS):
            line = xf[pl.ds(l, KPAD, stride=ROWS), :].astype(BF16)
            xc[i * per + l // sub, :, (l % sub) * lon_cols : (l % sub + 1) * lon_cols] = line
        acc = dot(xc[i * per], sel[0])
        for q in range(1, per):
            acc = acc + dot(xc[i * per + q], sel[q])
        strip[0, i] = acc[:, :128].astype(BF16)
        strip[1, i] = acc[:, 128:].astype(BF16)
        return carry

    for copy in x_in:
        copy.wait()
    lax.fori_loop(0, blocks, relayout, 0)
    side_moves = [
        send(strip.at[0], east, {"gy": left}),
        send(strip.at[1], west, {"gy": right}),
        send(strip.at[1, blocks - 1], corner.at[0], {"gx": down, "gy": right}),
        send(strip.at[0, blocks - 1], corner.at[1], {"gx": down, "gy": left}),
        send(strip.at[1, 0], corner.at[2], {"gx": up, "gy": right}),
        send(strip.at[0, 0], corner.at[3], {"gx": up, "gy": left}),
    ]

    sender = send_ref[:, own(gz, mine)]
    lon_total = gy_n * lon_cols
    rl = sender // lon_total - gx * lat_rows + HALO
    cl = sender % lon_total - gy * lon_cols + HALO + lon_total
    cl = cl % lon_total
    cells = lat_rows * lon_cols
    base_n, base_s = cells, cells + HALO * lon_cols
    base_w = cells + 2 * HALO * lon_cols
    base_e = base_w + HALO * lat_rows
    base_c = base_e + HALO * lat_rows
    is_n, is_s = rl < HALO, rl >= lat_rows + HALO
    is_w, is_e = cl < HALO, cl >= lon_cols + HALO
    c_in = jnp.where(is_w, cl, cl - (lon_cols + HALO))
    middle = jnp.where(
        is_n, base_n + rl * lon_cols,
        jnp.where(is_s, base_s + (rl - lat_rows - HALO) * lon_cols, (rl - HALO) * lon_cols),
    ) + cl - HALO
    aside = jnp.where(is_w, base_w, base_e) + (rl - HALO) * HALO + c_in
    cornered = (
        base_c
        + jnp.where(is_n, 0, 2 * 128)
        + jnp.where(is_w, 0, 128)
        + jnp.where(is_n, (rl + ROWS - HALO) * HALO, (rl - lat_rows - HALO) * HALO)
        + c_in
    )
    place_of = jnp.where(is_w | is_e, jnp.where(is_n | is_s, cornered, aside), middle)

    def onehot(base, size):
        ids = lax.broadcasted_iota(jnp.int32, (size, mine), 0)
        return jnp.where(ids == place_of - base, 1.0, 0.0).astype(BF16)

    for copy in w2r_in:
        copy.wait()
    gath[...] = jnp.zeros_like(gath)
    gain_own = cols[0, own(gz), :]

    def embed(i, carry):
        def step(q, inner):
            t = i * per + q
            xt = xc[t]
            hidden = half_silu(dot(w1p[...], xt))
            c, inv = centred(dot(w2r_v[...], hidden))
            out = c[:share] * inv * wide(gain_own, sub)
            for l in range(sub):
                outf[pl.ds(q * sub + l, share, stride=ROWS), :] = out[:, l * lon_cols : (l + 1) * lon_cols]
            gath[...] += dot(xt, onehot(t * TILE, TILE))
            return inner

        lax.fori_loop(0, per, step, 0)
        ob[i] = outf[...].reshape(share, ROWS, lon_cols).astype(BF16)
        pltpu.make_async_copy(ob.at[i], out_grid.at[:, pl.ds(i * ROWS, ROWS), :], bar_unused.at[i]).start()
        return carry

    lax.fori_loop(0, blocks, embed, 0)

    live = count_ref[0, 0]
    tile = gx * gy_n + gy
    node_ids = lax.broadcasted_iota(jnp.int32, (nodes, slots), 0)
    slot_ids = lax.broadcasted_iota(jnp.int32, (nodes, slots), 1)
    near = recv_ref[...] - tile * nodes
    pick = jnp.where((node_ids == near) & (slot_ids < live), 1.0, 0.0).astype(BF16)
    eown_in.wait()
    edge_sum = dot_nt(e_own[...], pick)
    degree = dot_nt(jnp.ones((8, slots), BF16), pick)[0:1, :]
    my_near = recv_ref[:, own(gz, mine)] - tile * nodes
    my_ids = lax.broadcasted_iota(jnp.int32, (nodes, mine), 0)
    my_slots = lax.broadcasted_iota(jnp.int32, (nodes, mine), 1) + gz * mine
    my_pick = jnp.where((my_ids == my_near) & (my_slots < live), 1.0, 0.0).astype(BF16)

    for copy in row_moves:
        copy.wait()
    half = KPAD * HALO
    xf[pl.ds(channels * HALO, (KPAD - channels) * HALO), :] = pad_values[0 : (KPAD - channels) * HALO] * 0.0 + jnp.where(
        lax.broadcasted_iota(jnp.int32, ((KPAD - channels) * HALO, 128), 0) < 3 * HALO, 1.0, 0.0
    ).astype(F32)
    for n, ref in enumerate((north, south)):
        xf[pl.ds(0, channels * HALO), :] = ref[...].astype(F32).reshape(channels * HALO, lon_cols)
        for l in range(HALO):
            xh[n, :, l * lon_cols : (l + 1) * lon_cols] = xf[pl.ds(l, KPAD, stride=HALO), :].astype(BF16)
    acc = gath[...]
    wing = HALO * lon_cols
    acc = acc + dot(xh[0], onehot(base_n, wing)) + dot(xh[1], onehot(base_s, wing))
    for copy in side_moves:
        copy.wait()
    for i in range(blocks):
        acc = acc + dot(west[i], onehot(base_w + i * 128, 128)) + dot(east[i], onehot(base_e + i * 128, 128))
    for i in range(4):
        acc = acc + dot(corner[i], onehot(base_c + i * 128, 128))
    picked = acc.astype(BF16)

    w2_in.wait()
    c, inv = centred(dot(w2_v[...], half_silu(dot(w1p[...], picked))))
    sender_latent = (c * inv * wide(cols[0], mine // 128)).astype(BF16)

    ew1_in.wait()
    mesh_in.wait()
    for copy in mesh_moves:
        copy.wait()
    mesh_cols = dot(mesh_full[...], my_pick).astype(BF16)
    pre = dot(ew1_v[:, latent : 2 * latent], sender_latent) + dot(ew1_v[:, 2 * latent :], mesh_cols)
    edge_in.wait()
    for copy in edge_moves:
        copy.wait()
    pre = pre + dot(ew1_v[:, :latent], edges[...])
    hidden = half_silu((pre + wide(cols[1], mine // 128)) * 0.5)
    ew2_in.wait()
    c, inv = centred(dot(ew2_v[...], hidden))
    tot[...] = dot_nt((c * inv).astype(BF16), my_pick)
    for k in range(gz_n):
        tb[k] = tot[k * share : (k + 1) * share, :].astype(BF16)
    sum_moves = [send(tb.at[peers[d]], tr.at[d], {"gz": peers[d]}) for d in order]
    total = tot[own(gz), :]
    scale = 1.0 / jnp.maximum(degree, 1.0)
    bias_own = wide(cols[3, own(gz), :], nodes // 128)
    gain_m = wide(cols[2, own(gz), :], nodes // 128)
    mown_in.wait()
    known = edge_sum + bias_own * degree
    base = mesh_own[...].astype(F32)
    for copy in sum_moves:
        copy.wait()
    for d in range(gz_n - 1):
        total = total + tr[d].astype(F32)
    out_mesh[...] = (base + (known + gain_m * total) * scale).astype(BF16)
    for i in range(blocks):
        pltpu.make_async_copy(ob.at[i], out_grid.at[:, pl.ds(i * ROWS, ROWS), :], bar_unused.at[i]).wait()


def on_device(
    sizes, grid_inputs, embed_w1, embed_b1, embed_w2, embed_gain, edge_w1, edge_b1, edge_w2,
    message_gain, message_bias, mesh_latent, edge_latent, senders, receivers, edge_counts,
):
    channels, lat_rows, lon_cols = grid_inputs.shape
    latent = embed_w2.shape[0]
    share, nodes, slots = mesh_latent.shape[0], mesh_latent.shape[3], edge_latent.shape[3]
    gz_n = sizes[2]
    mine = slots // gz_n
    blocks = lat_rows // ROWS
    tiles = lat_rows * lon_cols // TILE
    per = blocks and tiles // blocks
    anyspace = pl.BlockSpec(memory_space=pl.ANY)
    vmem = pl.BlockSpec(memory_space=pltpu.VMEM)
    smem = pl.BlockSpec(memory_space=pltpu.SMEM)
    V = pltpu.VMEM
    n_local = blocks + 1 + gz_n + 7
    n_wire = 3 * (gz_n - 1) + 8
    mesh_out, grid_out = pl.pallas_call(
        functools.partial(kernel, sizes),
        out_shape=(
            jax.ShapeDtypeStruct((share, nodes), BF16),
            jax.ShapeDtypeStruct((share, lat_rows, lon_cols), BF16),
        ),
        in_specs=[anyspace] * 5 + [vmem] * 5 + [anyspace] * 2 + [vmem] * 2 + [smem],
        out_specs=(vmem, anyspace),
        scratch_shapes=[
            V((blocks, channels, ROWS, lon_cols), BF16),
            V((channels, latent), BF16),
            V((latent, latent), BF16),
            V((latent, latent), BF16),
            V((latent, 3 * latent), BF16),
            V((latent, latent), BF16),
            V((share, slots), BF16),
            V((share, nodes), BF16),
            V((latent, mine), BF16),
            V((latent, nodes), BF16),
            V((channels, HALO, lon_cols), BF16),
            V((channels, HALO, lon_cols), BF16),
            V((blocks, KPAD, 128), BF16),
            V((blocks, KPAD, 128), BF16),
            V((4, KPAD, 128), BF16),
            V((KPAD * ROWS, lon_cols), F32),
            V((tiles, KPAD, TILE), BF16),
            V((2, KPAD, HALO * lon_cols), BF16),
            V((256, latent), F32),
            V((latent, KPAD), BF16),
            V((4, latent, 128), F32),
            V((per, TILE, 256), BF16),
            V((2, blocks, KPAD, 128), BF16),
            V((KPAD, mine), F32),
            V((share * ROWS, lon_cols), F32),
            V((blocks, share, ROWS, lon_cols), BF16),
            V((latent, nodes), F32),
            V((gz_n, share, nodes), BF16),
            V((gz_n - 1, share, nodes), BF16),
            pltpu.SemaphoreType.DMA((n_local,)),
            pltpu.SemaphoreType.DMA((n_wire,)),
            pltpu.SemaphoreType.DMA((n_wire,)),
            pltpu.SemaphoreType.DMA((blocks,)),
        ],
        compiler_params=pltpu.CompilerParams(
            collective_id=0, has_side_effects=True, vmem_limit_bytes=56 * 1024 * 1024
        ),
    )(
        grid_inputs, embed_w1.T, embed_w2, edge_w1, edge_w2,
        embed_b1.reshape(1, latent), embed_gain.reshape(1, latent), edge_b1.reshape(1, latent),
        message_gain.reshape(1, latent), message_bias.reshape(1, latent),
        mesh_latent.reshape(share, nodes), edge_latent.reshape(share, slots),
        senders.reshape(1, slots), receivers.reshape(1, slots), edge_counts,
    )
    return mesh_out.reshape(share, 1, 1, nodes), grid_out


def solution(mesh):
    sizes = (mesh.shape["gx"], mesh.shape["gy"], mesh.shape["gz"])
    return jax.shard_map(
        functools.partial(on_device, sizes),
        mesh=mesh,
        in_specs=(
            P(None, "gx", "gy"), P(), P(), P(), P(), P(), P(), P(), P(), P(),
            P("gz", "gx", "gy", None), P("gz", "gx", "gy", None),
            P("gx", "gy", None), P("gx", "gy", None), P("gx", "gy"),
        ),
        out_specs=(P("gz", "gx", "gy", None), P("gz", "gx", "gy")),
        check_vma=False,
    )
```

time: 137 us -> 58.2 us (0.42)
  the two profiles are of different devices: /device:TPU:32 before, /device:TPU:1 now
where the time goes in v1:
time: 58.2 us; the launch traced here: 58 us
  Pallas kernels  52.1 us (90%)
  local copies, waits for them, and re-layouts  4.55 us (8%)
  between operations  1.29 us (2%)
    pallas_call x1, Pallas kernels, on_device(): pl.pallas_call(functools.partial(kernel, sizes), out_shape=(jax.ShapeDtyp...  52.1 us
    unnamed x2, local copies, waits for them, and re-layouts  4.55 us

profile of v1, /device:TPU:1, one launch (start us, length us, event | category | flops | bytes accessed | tf_op | source)
XLA Modules:
  0.0 58.0 jit_solution(5839579018869898820)
XLA Ops:
  1.3 52.1 %shard_map.158 = (bf16[128,256]{1,0:T(8,128)(2,1)}, bf16[128,64,128]{2,1,0:T(8,128)(2,1)}) custom-call(bf16[186,64,128]{2,1,0:T(8,128)(2,1)} %x_hbm.1, bf16[186,512]{1,0:T(8,128)(2,1)} %bitcast.12, bf16[512,512]{1,0:T(8,128)(2,1)} %w2_hbm.1, bf16[512,1536]{1,0:T(8,128)(2,1)} %ew1_hbm.1, bf16[512,512]{1,0:T(8,128)(2,1)} %ew2_hbm.1, f32[1,512]{1,0:T(1,128)} %bitcast.17, ...), custom_call_target="tpu_custom_call" | custom-call | tf_op jit(solution)/shard_map/pallas_call | solution.py:316
  53.4 1.5 %copy.20 = bf16[128,1,1,256]{3,0,2,1:T(8,128)(2,1)} copy(bf16[128,1,1,256]{3,0,2,1:T(8,128)(2,1)} %bitcast.14) | data formatting | bytes 131072
  54.9 3.1 %copy.21 = bf16[128,64,128]{2,1,0:T(8,128)(2,1)} copy(bf16[128,64,128]{2,1,0:T(8,128)(2,1)} %get-tuple-element.9) | data formatting | bytes 4194304

commit v2 on v1

--- a/solution.py
+++ b/solution.py
@@ -9,9 +9,11 @@
 
 HALO = 8
 EPS = 1e-05
+FILL = (2, 4, 4, 7)
 F32 = jnp.float32
 BF16 = jnp.bfloat16
 TILE = 512
+PARTS = 2
 ROWS = 16
 KPAD = 192
 
@@ -44,11 +46,12 @@
     x_hbm, w1t_hbm, w2_hbm, ew1_hbm, ew2_hbm,
     b1_ref, gain_ref, eb1_ref, mgain_ref, mbias_ref,
     mesh_hbm, edge_hbm, send_ref, recv_ref, count_ref,
-    out_mesh, out_grid,
+    out_mesh, out_blocks,
     x_v, w1t_v, w2_v, w2r_v, ew1_v, ew2_v, e_own, mesh_own, edges, mesh_full,
     north, south, west, east, corner,
     xf, xc, xh, w1f, w1p, cols, sel, strip, gath, outf, ob, tot, tb, tr,
-    local, wsend, wrecv, bar_unused,
+    hid_a, hid_b, pre_s, pick_s,
+    local, wsend, wrecv, leave,
 ):
     gx_n, gy_n, gz_n = sizes
     channels, lat_rows, lon_cols = x_hbm.shape
@@ -65,7 +68,12 @@
 
     places = [{"gz": p} for p in peers]
     places += [{"gx": up}, {"gx": down}, {"gy": left}, {"gy": right}]
-    places += [{"gx": a, "gy": b} for a in (up, down) for b in (left, right)]
+    y, z_lo = lax.rem(gy, 4), gy // 4
+    lean_e = jnp.where(y == 3, jnp.where(z_lo == 0, gz_n - 1, 1), 0)
+    lean_w = jnp.where(y == 0, jnp.where(z_lo == 0, gz_n - 1, 1), 0)
+    east_place = {"gy": right, "gz": lax.rem(gz + lean_e, gz_n)}
+    west_place = {"gy": left, "gz": lax.rem(gz + lean_w, gz_n)}
+    places += [east_place, west_place]
     barrier = pltpu.get_barrier_semaphore()
     for place in places:
         pl.semaphore_signal(barrier, inc=1, device_id=place, device_id_type=pl.DeviceIdType.MESH)
@@ -88,7 +96,10 @@
         for j in range(gz_n)
     ]
     w2_in = bring(w2_hbm, w2_v)
-    edge_in = bring(edge_hbm.at[:, own(gz, mine)], edges.at[own(gz), :])
+    part = mine // PARTS
+    edge_in = [
+        bring(edge_hbm.at[:, own(gz * PARTS + b, part)], edges.at[b, own(gz), :]) for b in range(PARTS)
+    ]
     mesh_in = bring(mesh_hbm, mesh_full.at[own(gz), :])
     mown_in = bring(mesh_hbm, mesh_own)
     eown_in = bring(edge_hbm, e_own)
@@ -125,15 +136,10 @@
 
     order = [1, 0, 2] if gz_n == 4 else list(range(gz_n - 1))
     mesh_moves = [send(mesh_hbm, mesh_full.at[own(gz), :], {"gz": peers[d]}) for d in order]
-    edge_moves = [
-        send(edge_hbm.at[:, own(peers[d], mine)], edges.at[own(gz), :], {"gz": peers[d]})
-        for d in order
-    ]
     row_moves = [
         send(x_hbm.at[:, pl.ds(0, HALO), :], south, {"gx": up}),
         send(x_hbm.at[:, pl.ds(lat_rows - HALO, HALO), :], north, {"gx": down}),
     ]
-
     sub = TILE // lon_cols
     for q in range(ROWS // sub):
         k = lax.broadcasted_iota(jnp.int32, (TILE, 256), 0)
@@ -159,13 +165,19 @@
     for copy in x_in:
         copy.wait()
     lax.fori_loop(0, blocks, relayout, 0)
+    cut = blocks // 2
     side_moves = [
-        send(strip.at[0], east, {"gy": left}),
-        send(strip.at[1], west, {"gy": right}),
-        send(strip.at[1, blocks - 1], corner.at[0], {"gx": down, "gy": right}),
-        send(strip.at[0, blocks - 1], corner.at[1], {"gx": down, "gy": left}),
-        send(strip.at[1, 0], corner.at[2], {"gx": up, "gy": right}),
-        send(strip.at[0, 0], corner.at[3], {"gx": up, "gy": left}),
+        send(strip.at[0, pl.ds(0, cut)], east.at[pl.ds(0, cut)], {"gy": left}),
+        send(strip.at[1, pl.ds(0, cut)], west.at[pl.ds(0, cut)], {"gy": right}),
+        send(strip.at[0, pl.ds(cut, cut)], east.at[pl.ds(cut, cut)], west_place),
+        send(strip.at[1, pl.ds(cut, cut)], west.at[pl.ds(cut, cut)], east_place),
+    ]
+    edge_moves = [
+        [
+            send(edge_hbm.at[:, own(peers[d] * PARTS + b, part)], edges.at[b, own(gz), :], {"gz": peers[d]})
+            for d in order
+        ]
+        for b in range(PARTS)
     ]
 
     sender = send_ref[:, own(gz, mine)]
@@ -199,43 +211,73 @@
         ids = lax.broadcasted_iota(jnp.int32, (size, mine), 0)
         return jnp.where(ids == place_of - base, 1.0, 0.0).astype(BF16)
 
-    for copy in w2r_in:
-        copy.wait()
     gath[...] = jnp.zeros_like(gath)
-    gain_own = cols[0, own(gz), :]
-
-    def embed(i, carry):
-        def step(q, inner):
-            t = i * per + q
-            xt = xc[t]
-            hidden = half_silu(dot(w1p[...], xt))
-            c, inv = centred(dot(w2r_v[...], hidden))
-            out = c[:share] * inv * wide(gain_own, sub)
-            for l in range(sub):
-                outf[pl.ds(q * sub + l, share, stride=ROWS), :] = out[:, l * lon_cols : (l + 1) * lon_cols]
-            gath[...] += dot(xt, onehot(t * TILE, TILE))
-            return inner
-
-        lax.fori_loop(0, per, step, 0)
-        ob[i] = outf[...].reshape(share, ROWS, lon_cols).astype(BF16)
-        pltpu.make_async_copy(ob.at[i], out_grid.at[:, pl.ds(i * ROWS, ROWS), :], bar_unused.at[i]).start()
+
+    def gather(t, carry):
+        gath[...] += dot(xc[t], onehot(t * TILE, TILE))
         return carry
 
-    lax.fori_loop(0, blocks, embed, 0)
+    tiles = cells // TILE
+    lax.fori_loop(0, tiles, gather, 0)
 
     live = count_ref[0, 0]
     tile = gx * gy_n + gy
-    node_ids = lax.broadcasted_iota(jnp.int32, (nodes, slots), 0)
-    slot_ids = lax.broadcasted_iota(jnp.int32, (nodes, slots), 1)
-    near = recv_ref[...] - tile * nodes
-    pick = jnp.where((node_ids == near) & (slot_ids < live), 1.0, 0.0).astype(BF16)
-    eown_in.wait()
-    edge_sum = dot_nt(e_own[...], pick)
-    degree = dot_nt(jnp.ones((8, slots), BF16), pick)[0:1, :]
-    my_near = recv_ref[:, own(gz, mine)] - tile * nodes
-    my_ids = lax.broadcasted_iota(jnp.int32, (nodes, mine), 0)
-    my_slots = lax.broadcasted_iota(jnp.int32, (nodes, mine), 1) + gz * mine
-    my_pick = jnp.where((my_ids == my_near) & (my_slots < live), 1.0, 0.0).astype(BF16)
+    for b in range(PARTS):
+        near = recv_ref[:, own(gz * PARTS + b, part)] - tile * nodes
+        ids = lax.broadcasted_iota(jnp.int32, (nodes, part), 0)
+        spots = lax.broadcasted_iota(jnp.int32, (nodes, part), 1) + (gz * PARTS + b) * part
+        pick_s[b] = jnp.where((ids == near) & (spots < live), 1.0, 0.0).astype(BF16)
+
+    for copy in w2r_in:
+        copy.wait()
+    gain_own = cols[0, own(gz), :]
+    first = latent // 2
+
+    def layers(t_in, hid_out, hid_in, spot):
+        pieces = []
+        for r in range(2):
+            rows = slice(r * first, (r + 1) * first)
+            h = dot(w1p[rows, :], xc[t_in])
+            pieces.append(dot(w2r_v[rows, :], hid_in[...]))
+            hid_out[rows, :] = half_silu(h)
+            if r == 0:
+                shift = jnp.mean(pieces[0], axis=0, keepdims=True)
+                d = pieces[0] - shift
+                d_own = d[:share]
+                squares = jnp.sum(d * d, axis=0, keepdims=True)
+            else:
+                d = pieces[1] - shift
+                lean = jnp.sum(d, axis=0, keepdims=True) * (1.0 / latent)
+                squares = squares + jnp.sum(d * d, axis=0, keepdims=True)
+        spread = squares * (1.0 / latent) - lean * lean
+        out = (d_own - lean) * lax.rsqrt(spread + EPS) * wide(gain_own, sub)
+        for l in range(sub):
+            outf[pl.ds(spot * sub + l, share, stride=2 * sub), :] = out[:, l * lon_cols : (l + 1) * lon_cols]
+
+    def leaving(u):
+        return pltpu.make_async_copy(ob.at[u], out_blocks.at[u], leave.at[u])
+
+    def pair(u, carry):
+        layers(2 * u + 1, hid_b, hid_a, 0)
+        layers(jnp.minimum(2 * u + 2, tiles - 1), hid_a, hid_b, 1)
+        ob[u] = outf[...].reshape(share, 2 * sub, lon_cols).astype(BF16)
+        leaving(u).start()
+        return carry
+
+    def embed(start, stop):
+        lax.fori_loop(start, stop, pair, 0)
+
+    hid_a[...] = half_silu(dot(w1p[...], xc[0]))
+    stops = FILL + (tiles // 2,)
+    embed(0, stops[0])
+    for copy in side_moves:
+        copy.wait()
+    corner_moves = [
+        send(west.at[blocks - 1], corner.at[0], {"gx": down}),
+        send(east.at[blocks - 1], corner.at[1], {"gx": down}),
+        send(west.at[0], corner.at[2], {"gx": up}),
+        send(east.at[0], corner.at[3], {"gx": up}),
+    ]
 
     for copy in row_moves:
         copy.wait()
@@ -250,10 +292,13 @@
     acc = gath[...]
     wing = HALO * lon_cols
     acc = acc + dot(xh[0], onehot(base_n, wing)) + dot(xh[1], onehot(base_s, wing))
-    for copy in side_moves:
-        copy.wait()
     for i in range(blocks):
         acc = acc + dot(west[i], onehot(base_w + i * 128, 128)) + dot(east[i], onehot(base_e + i * 128, 128))
+    gath[...] = acc
+    embed(stops[0], stops[1])
+    for copy in corner_moves:
+        copy.wait()
+    acc = gath[...]
     for i in range(4):
         acc = acc + dot(corner[i], onehot(base_c + i * 128, 128))
     picked = acc.astype(BF16)
@@ -261,38 +306,71 @@
     w2_in.wait()
     c, inv = centred(dot(w2_v[...], half_silu(dot(w1p[...], picked))))
     sender_latent = (c * inv * wide(cols[0], mine // 128)).astype(BF16)
-
     ew1_in.wait()
+    for b in range(PARTS):
+        pre_s[b] = dot(ew1_v[:, latent : 2 * latent], sender_latent[:, b * part : (b + 1) * part]) + wide(
+            cols[1], part // 128
+        )
+
+    def edge_net(b):
+        edge_in[b].wait()
+        for copy in edge_moves[b]:
+            copy.wait()
+        pre = pre_s[b] + dot(ew1_v[:, :latent], edges[b])
+        c, inv = centred(dot(ew2_v[...], half_silu(pre * 0.5)))
+        part_sum = dot_nt((c * inv).astype(BF16), pick_s[b])
+        tot[...] = part_sum if b == 0 else tot[...] + part_sum
+
     mesh_in.wait()
     for copy in mesh_moves:
         copy.wait()
-    mesh_cols = dot(mesh_full[...], my_pick).astype(BF16)
-    pre = dot(ew1_v[:, latent : 2 * latent], sender_latent) + dot(ew1_v[:, 2 * latent :], mesh_cols)
-    edge_in.wait()
-    for copy in edge_moves:
-        copy.wait()
-    pre = pre + dot(ew1_v[:, :latent], edges[...])
-    hidden = half_silu((pre + wide(cols[1], mine // 128)) * 0.5)
+    for b in range(PARTS):
+        mesh_cols = dot(mesh_full[...], pick_s[b]).astype(BF16)
+        pre_s[b] += dot(ew1_v[:, 2 * latent :], mesh_cols)
     ew2_in.wait()
-    c, inv = centred(dot(ew2_v[...], hidden))
-    tot[...] = dot_nt((c * inv).astype(BF16), my_pick)
+    for b in range(PARTS):
+        embed(stops[b + 1], stops[b + 2])
+        edge_net(b)
     for k in range(gz_n):
         tb[k] = tot[k * share : (k + 1) * share, :].astype(BF16)
     sum_moves = [send(tb.at[peers[d]], tr.at[d], {"gz": peers[d]}) for d in order]
+
+    embed(stops[PARTS + 1], stops[PARTS + 2])
+    node_ids = lax.broadcasted_iota(jnp.int32, (nodes, slots), 0)
+    slot_ids = lax.broadcasted_iota(jnp.int32, (nodes, slots), 1)
+    pick = jnp.where((node_ids == recv_ref[...] - tile * nodes) & (slot_ids < live), 1.0, 0.0).astype(BF16)
+    eown_in.wait()
+    edge_sum = dot_nt(e_own[...], pick)
+    degree = dot_nt(jnp.ones((8, slots), BF16), pick)[0:1, :]
+    scale = 1.0 / jnp.maximum(degree, 1.0)
+    gain_m = wide(cols[2, own(gz), :], nodes // 128)
+    known = edge_sum + wide(cols[3, own(gz), :], nodes // 128) * degree
+    mown_in.wait()
     total = tot[own(gz), :]
-    scale = 1.0 / jnp.maximum(degree, 1.0)
-    bias_own = wide(cols[3, own(gz), :], nodes // 128)
-    gain_m = wide(cols[2, own(gz), :], nodes // 128)
-    mown_in.wait()
-    known = edge_sum + bias_own * degree
-    base = mesh_own[...].astype(F32)
     for copy in sum_moves:
         copy.wait()
     for d in range(gz_n - 1):
         total = total + tr[d].astype(F32)
-    out_mesh[...] = (base + (known + gain_m * total) * scale).astype(BF16)
-    for i in range(blocks):
-        pltpu.make_async_copy(ob.at[i], out_grid.at[:, pl.ds(i * ROWS, ROWS), :], bar_unused.at[i]).wait()
+    out_mesh[...] = (mesh_own[...].astype(F32) + (known + gain_m * total) * scale).astype(BF16)
+    for u in range(tiles // 2):
+        leaving(u).wait()
+
+
+def deliver(mesh_ref, blocks_hbm, out_mesh, out_grid, buf, sin, sout):
+    count, _, rows, _ = blocks_hbm.shape
+    ins = [pltpu.make_async_copy(blocks_hbm.at[u], buf.at[u], sin.at[u]) for u in range(count)]
+    outs = [
+        pltpu.make_async_copy(buf.at[u], out_grid.at[:, pl.ds(u * rows, rows), :], sout.at[u])
+        for u in range(count)
+    ]
+    for copy in ins:
+        copy.start()
+    out_mesh[...] = mesh_ref[...]
+    for came, goes in zip(ins, outs):
+        came.wait()
+        goes.start()
+    for copy in outs:
+        copy.wait()
 
 
 def on_device(
@@ -311,13 +389,14 @@
     vmem = pl.BlockSpec(memory_space=pltpu.VMEM)
     smem = pl.BlockSpec(memory_space=pltpu.SMEM)
     V = pltpu.VMEM
-    n_local = blocks + 1 + gz_n + 7
-    n_wire = 3 * (gz_n - 1) + 8
-    mesh_out, grid_out = pl.pallas_call(
+    n_local = blocks + 1 + gz_n + 6 + PARTS
+    n_wire = (2 + PARTS) * (gz_n - 1) + 10
+    pairs, out_rows = tiles // 2, 2 * TILE // lon_cols
+    mesh_out, grid_blocks = pl.pallas_call(
         functools.partial(kernel, sizes),
         out_shape=(
             jax.ShapeDtypeStruct((share, nodes), BF16),
-            jax.ShapeDtypeStruct((share, lat_rows, lon_cols), BF16),
+            jax.ShapeDtypeStruct((pairs, share, out_rows, lon_cols), BF16),
         ),
         in_specs=[anyspace] * 5 + [vmem] * 5 + [anyspace] * 2 + [vmem] * 2 + [smem],
         out_specs=(vmem, anyspace),
@@ -330,7 +409,7 @@
             V((latent, latent), BF16),
             V((share, slots), BF16),
             V((share, nodes), BF16),
-            V((latent, mine), BF16),
+            V((PARTS, latent, mine // PARTS), BF16),
             V((latent, nodes), BF16),
             V((channels, HALO, lon_cols), BF16),
             V((channels, HALO, lon_cols), BF16),
@@ -346,15 +425,19 @@
             V((per, TILE, 256), BF16),
             V((2, blocks, KPAD, 128), BF16),
             V((KPAD, mine), F32),
-            V((share * ROWS, lon_cols), F32),
-            V((blocks, share, ROWS, lon_cols), BF16),
+            V((share * out_rows, lon_cols), F32),
+            V((pairs, share, out_rows, lon_cols), BF16),
             V((latent, nodes), F32),
             V((gz_n, share, nodes), BF16),
             V((gz_n - 1, share, nodes), BF16),
+            V((latent, TILE), BF16),
+            V((latent, TILE), BF16),
+            V((PARTS, latent, mine // PARTS), F32),
+            V((PARTS, nodes, mine // PARTS), BF16),
             pltpu.SemaphoreType.DMA((n_local,)),
             pltpu.SemaphoreType.DMA((n_wire,)),
             pltpu.SemaphoreType.DMA((n_wire,)),
-            pltpu.SemaphoreType.DMA((blocks,)),
+            pltpu.SemaphoreType.DMA((pairs,)),
         ],
         compiler_params=pltpu.CompilerParams(
             collective_id=0, has_side_effects=True, vmem_limit_bytes=56 * 1024 * 1024
@@ -366,6 +449,20 @@
         mesh_latent.reshape(share, nodes), edge_latent.reshape(share, slots),
         senders.reshape(1, slots), receivers.reshape(1, slots), edge_counts,
     )
+    mesh_out, grid_out = pl.pallas_call(
+        deliver,
+        out_shape=(
+            jax.ShapeDtypeStruct((share, nodes), BF16),
+            jax.ShapeDtypeStruct((share, lat_rows, lon_cols), BF16),
+        ),
+        in_specs=[vmem, anyspace],
+        out_specs=(vmem, anyspace),
+        scratch_shapes=[
+            V((pairs, share, out_rows, lon_cols), BF16),
+            pltpu.SemaphoreType.DMA((pairs,)),
+            pltpu.SemaphoreType.DMA((pairs,)),
+        ],
+    )(mesh_out, grid_blocks)
     return mesh_out.reshape(share, 1, 1, nodes), grid_out
 
 

time: 58.2 us -> 49.1 us (0.84)
  the two profiles are of different devices: /device:TPU:1 before, /device:TPU:4 now
where the time goes in v2:
time: 49.1 us; the launch traced here: 48.9 us
  Pallas kernels  47.6 us (97%)
  between operations  1.29 us (3%)
    pallas_call x1, Pallas kernels, on_device(): pl.pallas_call(functools.partial(kernel, sizes), out_shape=(jax.ShapeDtyp...  43.7 us
    pallas_call x1, Pallas kernels, on_device(): pl.pallas_call(deliver, out_shape=(jax.ShapeDtypeStruct((share, nodes), B...  3.86 us

profile of v2, /device:TPU:4, one launch (start us, length us, event | category | flops | bytes accessed | tf_op | source)
XLA Modules:
  0.0 48.9 jit_solution(63338328225560357)
XLA Ops:
  1.3 43.7 %shard_map.158 = (bf16[128,256]{1,0:T(8,128)(2,1)}, bf16[8,128,8,128]{3,2,1,0:T(8,128)(2,1)}) custom-call(bf16[186,64,128]{2,1,0:T(8,128)(2,1)} %x_hbm.1, bf16[186,512]{1,0:T(8,128)(2,1)} %bitcast.12, bf16[512,512]{1,0:T(8,128)(2,1)} %w2_hbm.1, bf16[512,1536]{1,0:T(8,128)(2,1)} %ew1_hbm.1, bf16[512,512]{1,0:T(8,128)(2,1)} %ew2_hbm.1, f32[1,512]{1,0:T(1,128)} %bitcast.16, ...), custom_call_target="tpu_custom_call" | custom-call | tf_op jit(solution)/shard_map/pallas_call | solution.py:395
  45.0 3.9 %shard_map.159 = (bf16[128,256]{1,0:T(8,128)(2,1)}, bf16[128,64,128]{2,1,0:T(8,128)(2,1)}) custom-call(bf16[128,256]{1,0:T(8,128)(2,1)} %get-tuple-element.6.mesh_ref, bf16[8,128,8,128]{3,2,1,0:T(8,128)(2,1)} %get-tuple-element.7.blocks_hbm), custom_call_target="tpu_custom_call" | custom-call | tf_op jit(solution)/shard_map/pallas_call | solution.py:452

commit v3 on v2

--- a/solution.py
+++ b/solution.py
@@ -9,7 +9,7 @@
 
 HALO = 8
 EPS = 1e-05
-FILL = (2, 4, 4, 7)
+FILL = (5, 6, 6, 6)
 F32 = jnp.float32
 BF16 = jnp.bfloat16
 TILE = 512
@@ -44,14 +44,15 @@
 def kernel(
     sizes,
     x_hbm, w1t_hbm, w2_hbm, ew1_hbm, ew2_hbm,
-    b1_ref, gain_ref, eb1_ref, mgain_ref, mbias_ref,
-    mesh_hbm, edge_hbm, send_ref, recv_ref, count_ref,
+    b1_hbm, gain_hbm, eb1_hbm, mgain_hbm, mbias_hbm,
+    mesh_hbm, edge_hbm, send_hbm, recv_hbm, count_ref,
     out_mesh, out_blocks,
     x_v, w1t_v, w2_v, w2r_v, ew1_v, ew2_v, e_own, mesh_own, edges, mesh_full,
     north, south, west, east, corner,
-    xf, xc, xh, w1f, w1p, cols, sel, strip, gath, outf, ob, tot, tb, tr,
+    xf, xc, xh, w1f, w1p, cols, sel, strip, gath, outf, tot, tb, tr,
     hid_a, hid_b, pre_s, pick_s,
-    local, wsend, wrecv, leave,
+    vecs, send_ref, recv_ref,
+    local, wsend, wrecv,
 ):
     gx_n, gy_n, gz_n = sizes
     channels, lat_rows, lon_cols = x_hbm.shape
@@ -81,6 +82,7 @@
     def own(index, size=share):
         return pl.ds(pl.multiple_of(index * size, 128), size)
 
+    vec_hbm = (b1_hbm, gain_hbm, eb1_hbm, mgain_hbm, mbias_hbm)
     copies = []
 
     def bring(src, dst):
@@ -89,38 +91,10 @@
         copies.append(copy)
         return copy
 
+    w1_in = bring(w1t_hbm, w1t_v)
+    vec_in = [bring(ref, vecs.at[k]) for k, ref in enumerate(vec_hbm)]
     x_in = [bring(x_hbm.at[:, pl.ds(i * ROWS, ROWS), :], x_v.at[i]) for i in range(blocks)]
-    w1_in = bring(w1t_hbm, w1t_v)
-    w2r_in = [
-        bring(w2_hbm.at[own(lax.rem(gz + j, gz_n)), :], w2r_v.at[pl.ds(j * share, share), :])
-        for j in range(gz_n)
-    ]
-    w2_in = bring(w2_hbm, w2_v)
     part = mine // PARTS
-    edge_in = [
-        bring(edge_hbm.at[:, own(gz * PARTS + b, part)], edges.at[b, own(gz), :]) for b in range(PARTS)
-    ]
-    mesh_in = bring(mesh_hbm, mesh_full.at[own(gz), :])
-    mown_in = bring(mesh_hbm, mesh_own)
-    eown_in = bring(edge_hbm, e_own)
-    ew1_in = bring(ew1_hbm, ew1_v)
-    ew2_in = bring(ew2_hbm, ew2_v)
-
-    w1_in.wait()
-    w1f[...] = jnp.zeros_like(w1f)
-    w1f[0:channels, :] = w1t_v[...].astype(F32) * 0.5
-    half_b = b1_ref[...] * 0.5
-    for k in range(3):
-        piece = half_b.astype(BF16).astype(F32)
-        w1f[channels + k : channels + k + 1, :] = piece
-        half_b = half_b - piece
-    w1p[...] = jnp.transpose(w1f[...])[:, :KPAD].astype(BF16)
-    for k, ref in enumerate((gain_ref, eb1_ref, mgain_ref, mbias_ref)):
-        cols[k] = jnp.transpose(jnp.broadcast_to(ref[...], (128, latent)))
-    pad_rows = lax.broadcasted_iota(jnp.int32, ((KPAD - channels) * ROWS, 128), 0)
-    pad_values = jnp.where(pad_rows < 3 * ROWS, 1.0, 0.0).astype(F32)
-    xf[pl.ds(channels * ROWS, (KPAD - channels) * ROWS), :] = pad_values
-
     pl.semaphore_wait(barrier, len(places))
     sent = []
 
@@ -134,12 +108,34 @@
         sent.append(copy)
         return copy
 
-    order = [1, 0, 2] if gz_n == 4 else list(range(gz_n - 1))
-    mesh_moves = [send(mesh_hbm, mesh_full.at[own(gz), :], {"gz": peers[d]}) for d in order]
+    after, across, before = peers
+    mesh_moves = [send(mesh_hbm, mesh_full.at[own(gz), :], {"gz": p}) for p in (after, before)]
+
+    def send_edges(b, p):
+        return send(edge_hbm.at[:, own(p * PARTS + b, part)], edges.at[b, own(gz), :], {"gz": p})
+
+    edge_moves = [[], []]
     row_moves = [
         send(x_hbm.at[:, pl.ds(0, HALO), :], south, {"gx": up}),
         send(x_hbm.at[:, pl.ds(lat_rows - HALO, HALO), :], north, {"gx": down}),
     ]
+    w1_in.wait()
+    for copy in vec_in:
+        copy.wait()
+    w1f[...] = jnp.zeros_like(w1f)
+    w1f[0:channels, :] = w1t_v[...].astype(F32) * 0.5
+    half_b = vecs[0] * 0.5
+    for k in range(3):
+        piece = half_b.astype(BF16).astype(F32)
+        w1f[channels + k : channels + k + 1, :] = piece
+        half_b = half_b - piece
+    w1p[...] = jnp.transpose(w1f[...])[:, :KPAD].astype(BF16)
+    for k in range(4):
+        cols[k] = jnp.transpose(jnp.broadcast_to(vecs[k + 1], (128, latent)))
+    pad_rows = lax.broadcasted_iota(jnp.int32, ((KPAD - channels) * ROWS, 128), 0)
+    pad_values = jnp.where(pad_rows < 3 * ROWS, 1.0, 0.0).astype(F32)
+    xf[pl.ds(channels * ROWS, (KPAD - channels) * ROWS), :] = pad_values
+
     sub = TILE // lon_cols
     for q in range(ROWS // sub):
         k = lax.broadcasted_iota(jnp.int32, (TILE, 256), 0)
@@ -164,6 +160,21 @@
 
     for copy in x_in:
         copy.wait()
+    w2r_in = [
+        bring(w2_hbm.at[own(lax.rem(gz + j, gz_n)), :], w2r_v.at[pl.ds(j * share, share), :])
+        for j in range(gz_n)
+    ]
+    w2_in = bring(w2_hbm, w2_v)
+    index_in = [bring(send_hbm, send_ref), bring(recv_hbm, recv_ref)]
+    edge_in = [
+        bring(edge_hbm.at[:, own(gz * PARTS + b, part)], edges.at[b, own(gz), :]) for b in range(PARTS)
+    ]
+    mesh_in = bring(mesh_hbm, mesh_full.at[own(gz), :])
+    mown_in = bring(mesh_hbm, mesh_own)
+    eown_in = bring(edge_hbm, e_own)
+    ew1_in = bring(ew1_hbm, ew1_v)
+    ew2_in = bring(ew2_hbm, ew2_v)
+
     lax.fori_loop(0, blocks, relayout, 0)
     cut = blocks // 2
     side_moves = [
@@ -172,14 +183,9 @@
         send(strip.at[0, pl.ds(cut, cut)], east.at[pl.ds(cut, cut)], west_place),
         send(strip.at[1, pl.ds(cut, cut)], west.at[pl.ds(cut, cut)], east_place),
     ]
-    edge_moves = [
-        [
-            send(edge_hbm.at[:, own(peers[d] * PARTS + b, part)], edges.at[b, own(gz), :], {"gz": peers[d]})
-            for d in order
-        ]
-        for b in range(PARTS)
-    ]
-
+    edge_moves[0] += [send_edges(0, p) for p in (across, after, before)]
+    for copy in index_in:
+        copy.wait()
     sender = send_ref[:, own(gz, mine)]
     lon_total = gy_n * lon_cols
     rl = sender // lon_total - gx * lat_rows + HALO
@@ -214,11 +220,21 @@
     gath[...] = jnp.zeros_like(gath)
 
     def gather(t, carry):
-        gath[...] += dot(xc[t], onehot(t * TILE, TILE))
+        found = dot(xc[t * per], onehot(t * per * TILE, TILE))
+        for q in range(1, per):
+            found = found + dot(xc[t * per + q], onehot((t * per + q) * TILE, TILE))
+        gath[...] += found
         return carry
 
     tiles = cells // TILE
-    lax.fori_loop(0, tiles, gather, 0)
+    lax.fori_loop(0, blocks, gather, 0)
+
+    for copy in mesh_moves:
+        copy.wait()
+    upper = mesh_full.at[pl.ds(pl.multiple_of(before * share, 128), share // 2), :]
+    lower = mesh_full.at[pl.ds(pl.multiple_of(after * share + share // 2, 64), share // 2), :]
+    mesh_moves = [send(upper, upper, {"gz": after}), send(lower, lower, {"gz": before})]
+    edge_moves[1] = [send_edges(1, p) for p in (across, after, before)]
 
     live = count_ref[0, 0]
     tile = gx * gy_n + gy
@@ -233,7 +249,9 @@
     gain_own = cols[0, own(gz), :]
     first = latent // 2
 
-    def layers(t_in, hid_out, hid_in, spot):
+    lines = share * 2 * sub
+
+    def layers(t_in, hid_out, hid_in, spot, base):
         pieces = []
         for r in range(2):
             rows = slice(r * first, (r + 1) * first)
@@ -252,22 +270,24 @@
         spread = squares * (1.0 / latent) - lean * lean
         out = (d_own - lean) * lax.rsqrt(spread + EPS) * wide(gain_own, sub)
         for l in range(sub):
-            outf[pl.ds(spot * sub + l, share, stride=2 * sub), :] = out[:, l * lon_cols : (l + 1) * lon_cols]
-
-    def leaving(u):
-        return pltpu.make_async_copy(ob.at[u], out_blocks.at[u], leave.at[u])
+            outf[pl.ds(base + spot * sub + l, share, stride=2 * sub), :] = out[:, l * lon_cols : (l + 1) * lon_cols]
+
+    def settle(u):
+        base = pl.multiple_of(lax.rem(u, 2) * lines, lines)
+        out_blocks[u] = outf[pl.ds(base, lines), :].reshape(share, 2 * sub, lon_cols).astype(BF16)
 
     def pair(u, carry):
-        layers(2 * u + 1, hid_b, hid_a, 0)
-        layers(jnp.minimum(2 * u + 2, tiles - 1), hid_a, hid_b, 1)
-        ob[u] = outf[...].reshape(share, 2 * sub, lon_cols).astype(BF16)
-        leaving(u).start()
+        settle(jnp.maximum(u - 1, 0))
+        base = lax.rem(u, 2) * lines
+        layers(2 * u + 1, hid_b, hid_a, 0, base)
+        layers(jnp.minimum(2 * u + 2, tiles - 1), hid_a, hid_b, 1, base)
         return carry
 
     def embed(start, stop):
         lax.fori_loop(start, stop, pair, 0)
 
     hid_a[...] = half_silu(dot(w1p[...], xc[0]))
+    outf[...] = jnp.zeros_like(outf)
     stops = FILL + (tiles // 2,)
     embed(0, stops[0])
     for copy in side_moves:
@@ -331,11 +351,18 @@
     for b in range(PARTS):
         embed(stops[b + 1], stops[b + 2])
         edge_net(b)
-    for k in range(gz_n):
-        tb[k] = tot[k * share : (k + 1) * share, :].astype(BF16)
-    sum_moves = [send(tb.at[peers[d]], tr.at[d], {"gz": peers[d]}) for d in order]
-
-    embed(stops[PARTS + 1], stops[PARTS + 2])
+    half = share // 2
+
+    def sums(p, k):
+        return tot[pl.ds(pl.multiple_of(p * share + k * half, 64), half), :]
+
+    for k in range(2):
+        tb[k] = sums(across, k).astype(BF16)
+    tb[2] = sums(after, 1).astype(BF16)
+    tb[3] = sums(before, 0).astype(BF16)
+    relays = [send(tb.at[0], tr.at[0], {"gz": after}), send(tb.at[1], tr.at[1], {"gz": before})]
+    sum_moves = [send(tb.at[2], tr.at[2], {"gz": after}), send(tb.at[3], tr.at[3], {"gz": before})]
+
     node_ids = lax.broadcasted_iota(jnp.int32, (nodes, slots), 0)
     slot_ids = lax.broadcasted_iota(jnp.int32, (nodes, slots), 1)
     pick = jnp.where((node_ids == recv_ref[...] - tile * nodes) & (slot_ids < live), 1.0, 0.0).astype(BF16)
@@ -346,29 +373,30 @@
     gain_m = wide(cols[2, own(gz), :], nodes // 128)
     known = edge_sum + wide(cols[3, own(gz), :], nodes // 128) * degree
     mown_in.wait()
-    total = tot[own(gz), :]
+    for copy in relays:
+        copy.wait()
+    tb[4] = (sums(after, 0) + tr[0].astype(F32)).astype(BF16)
+    tb[5] = (sums(before, 1) + tr[1].astype(F32)).astype(BF16)
+    sum_moves += [send(tb.at[4], tr.at[4], {"gz": after}), send(tb.at[5], tr.at[5], {"gz": before})]
+    embed(stops[PARTS + 1], stops[PARTS + 2])
+    settle(tiles // 2 - 1)
     for copy in sum_moves:
         copy.wait()
-    for d in range(gz_n - 1):
-        total = total + tr[d].astype(F32)
+    total = tot[own(gz), :] + jnp.concatenate(
+        [tr[4].astype(F32) + tr[3].astype(F32), tr[2].astype(F32) + tr[5].astype(F32)], axis=0
+    )
     out_mesh[...] = (mesh_own[...].astype(F32) + (known + gain_m * total) * scale).astype(BF16)
-    for u in range(tiles // 2):
-        leaving(u).wait()
-
-
-def deliver(mesh_ref, blocks_hbm, out_mesh, out_grid, buf, sin, sout):
-    count, _, rows, _ = blocks_hbm.shape
-    ins = [pltpu.make_async_copy(blocks_hbm.at[u], buf.at[u], sin.at[u]) for u in range(count)]
+
+
+def deliver(mesh_ref, blocks_ref, out_mesh, out_grid, leave):
+    count, _, rows, _ = blocks_ref.shape
     outs = [
-        pltpu.make_async_copy(buf.at[u], out_grid.at[:, pl.ds(u * rows, rows), :], sout.at[u])
+        pltpu.make_async_copy(blocks_ref.at[u], out_grid.at[:, pl.ds(u * rows, rows), :], leave.at[u])
         for u in range(count)
     ]
-    for copy in ins:
+    outs.append(pltpu.make_async_copy(mesh_ref, out_mesh, leave.at[count]))
+    for copy in outs:
         copy.start()
-    out_mesh[...] = mesh_ref[...]
-    for came, goes in zip(ins, outs):
-        came.wait()
-        goes.start()
     for copy in outs:
         copy.wait()
 
@@ -389,17 +417,17 @@
     vmem = pl.BlockSpec(memory_space=pltpu.VMEM)
     smem = pl.BlockSpec(memory_space=pltpu.SMEM)
     V = pltpu.VMEM
-    n_local = blocks + 1 + gz_n + 6 + PARTS
-    n_wire = (2 + PARTS) * (gz_n - 1) + 10
+    n_local = blocks + 1 + gz_n + 6 + PARTS + 7
+    n_wire = PARTS * (gz_n - 1) + 20
     pairs, out_rows = tiles // 2, 2 * TILE // lon_cols
     mesh_out, grid_blocks = pl.pallas_call(
         functools.partial(kernel, sizes),
         out_shape=(
-            jax.ShapeDtypeStruct((share, nodes), BF16),
-            jax.ShapeDtypeStruct((pairs, share, out_rows, lon_cols), BF16),
+            pltpu.VMEM((share, nodes), BF16),
+            pltpu.VMEM((pairs, share, out_rows, lon_cols), BF16),
         ),
-        in_specs=[anyspace] * 5 + [vmem] * 5 + [anyspace] * 2 + [vmem] * 2 + [smem],
-        out_specs=(vmem, anyspace),
+        in_specs=[anyspace] * 14 + [smem],
+        out_specs=(vmem, vmem),
         scratch_shapes=[
             V((blocks, channels, ROWS, lon_cols), BF16),
             V((channels, latent), BF16),
@@ -425,19 +453,20 @@
             V((per, TILE, 256), BF16),
             V((2, blocks, KPAD, 128), BF16),
             V((KPAD, mine), F32),
-            V((share * out_rows, lon_cols), F32),
-            V((pairs, share, out_rows, lon_cols), BF16),
+            V((2 * share * out_rows, lon_cols), F32),
             V((latent, nodes), F32),
-            V((gz_n, share, nodes), BF16),
-            V((gz_n - 1, share, nodes), BF16),
+            V((6, share // 2, nodes), BF16),
+            V((6, share // 2, nodes), BF16),
             V((latent, TILE), BF16),
             V((latent, TILE), BF16),
             V((PARTS, latent, mine // PARTS), F32),
             V((PARTS, nodes, mine // PARTS), BF16),
+            V((5, 1, latent), F32),
+            V((1, slots), jnp.int32),
+            V((1, slots), jnp.int32),
             pltpu.SemaphoreType.DMA((n_local,)),
             pltpu.SemaphoreType.DMA((n_wire,)),
             pltpu.SemaphoreType.DMA((n_wire,)),
-            pltpu.SemaphoreType.DMA((pairs,)),
         ],
         compiler_params=pltpu.CompilerParams(
             collective_id=0, has_side_effects=True, vmem_limit_bytes=56 * 1024 * 1024
@@ -455,14 +484,13 @@
             jax.ShapeDtypeStruct((share, nodes), BF16),
             jax.ShapeDtypeStruct((share, lat_rows, lon_cols), BF16),
         ),
-        in_specs=[vmem, anyspace],
-        out_specs=(vmem, anyspace),
-        scratch_shapes=[
-            V((pairs, share, out_rows, lon_cols), BF16),
-            pltpu.SemaphoreType.DMA((pairs,)),
-            pltpu.SemaphoreType.DMA((pairs,)),
-        ],
-    )(mesh_out, grid_blocks)
+        in_specs=[vmem, vmem],
+        out_specs=(anyspace, anyspace),
+        scratch_shapes=[pltpu.SemaphoreType.DMA((pairs + 1,))],
+    )(
+        pltpu.with_memory_space_constraint(mesh_out, pltpu.VMEM),
+        pltpu.with_memory_space_constraint(grid_blocks, pltpu.VMEM),
+    )
     return mesh_out.reshape(share, 1, 1, nodes), grid_out
 
 

time: 49.1 us -> 43.4 us (0.88)
  Pallas kernels: 47.6 us -> 41.8 us
    pallas_call x1, Pallas kernels: 43.7 us -> 40.4 us  [on_device(): pl.pallas_call(functools.partial(kernel, sizes), out_shape=(pltpu.VMEM((s...]
    pallas_call x1, Pallas kernels: 3.86 us -> 1.4 us  [on_device(): pl.pallas_call(deliver, out_shape=(jax.ShapeDtypeStruct((share, nodes), B...]
where the time goes in v3:
time: 43.4 us; the launch traced here: 43.1 us
  Pallas kernels  41.8 us (96%)
  between operations  1.29 us (3%)
    pallas_call x1, Pallas kernels, on_device(): pl.pallas_call(functools.partial(kernel, sizes), out_shape=(pltpu.VMEM((s...  40.4 us
    pallas_call x1, Pallas kernels, on_device(): pl.pallas_call(deliver, out_shape=(jax.ShapeDtypeStruct((share, nodes), B...  1.4 us

profile of v3, /device:TPU:4, one launch (start us, length us, event | category | flops | bytes accessed | tf_op | source)
XLA Modules:
  0.0 43.1 jit_solution(7877499983269046104)
XLA Ops:
  1.3 40.4 %shard_map.158 = (bf16[128,256]{1,0:T(8,128)(2,1)S(1)}, bf16[8,128,8,128]{3,2,1,0:T(8,128)(2,1)S(1)}) custom-call(bf16[186,64,128]{2,1,0:T(8,128)(2,1)} %x_hbm.1, bf16[186,512]{1,0:T(8,128)(2,1)} %bitcast.12, bf16[512,512]{1,0:T(8,128)(2,1)} %w2_hbm.1, bf16[512,1536]{1,0:T(8,128)(2,1)} %ew1_hbm.1, bf16[512,512]{1,0:T(8,128)(2,1)} %ew2_hbm.1, ...), custom_call_target="tpu_custom_call" | custom-call | tf_op jit(solution)/shard_map/pallas_call | solution.py:423
  41.7 1.4 %shard_map.159 = (bf16[128,256]{1,0:T(8,128)(2,1)}, bf16[128,64,128]{2,1,0:T(8,128)(2,1)}) custom-call(bf16[128,256]{1,0:T(8,128)(2,1)S(1)} %get-tuple-element.6.mesh_ref, bf16[8,128,8,128]{3,2,1,0:T(8,128)(2,1)S(1)} %get-tuple-element.7.blocks_ref), custom_call_target="tpu_custom_call" | custom-call | tf_op jit(solution)/shard_map/pallas_call | solution.py:481

commit v4 on v3

--- a/solution.py
+++ b/solution.py
@@ -9,7 +9,7 @@
 
 HALO = 8
 EPS = 1e-05
-FILL = (5, 6, 6, 6)
+FILL = (4, 6, 6, 6)
 F32 = jnp.float32
 BF16 = jnp.bfloat16
 TILE = 512
@@ -94,6 +94,7 @@
     w1_in = bring(w1t_hbm, w1t_v)
     vec_in = [bring(ref, vecs.at[k]) for k, ref in enumerate(vec_hbm)]
     x_in = [bring(x_hbm.at[:, pl.ds(i * ROWS, ROWS), :], x_v.at[i]) for i in range(blocks)]
+    index_in = [bring(send_hbm, send_ref), bring(recv_hbm, recv_ref)]
     part = mine // PARTS
     pl.semaphore_wait(barrier, len(places))
     sent = []
@@ -160,21 +161,6 @@
 
     for copy in x_in:
         copy.wait()
-    w2r_in = [
-        bring(w2_hbm.at[own(lax.rem(gz + j, gz_n)), :], w2r_v.at[pl.ds(j * share, share), :])
-        for j in range(gz_n)
-    ]
-    w2_in = bring(w2_hbm, w2_v)
-    index_in = [bring(send_hbm, send_ref), bring(recv_hbm, recv_ref)]
-    edge_in = [
-        bring(edge_hbm.at[:, own(gz * PARTS + b, part)], edges.at[b, own(gz), :]) for b in range(PARTS)
-    ]
-    mesh_in = bring(mesh_hbm, mesh_full.at[own(gz), :])
-    mown_in = bring(mesh_hbm, mesh_own)
-    eown_in = bring(edge_hbm, e_own)
-    ew1_in = bring(ew1_hbm, ew1_v)
-    ew2_in = bring(ew2_hbm, ew2_v)
-
     lax.fori_loop(0, blocks, relayout, 0)
     cut = blocks // 2
     side_moves = [
@@ -184,6 +170,20 @@
         send(strip.at[1, pl.ds(cut, cut)], west.at[pl.ds(cut, cut)], east_place),
     ]
     edge_moves[0] += [send_edges(0, p) for p in (across, after, before)]
+    w2r_in = [
+        bring(w2_hbm.at[own(lax.rem(gz + j, gz_n)), :], w2r_v.at[pl.ds(j * share, share), :])
+        for j in range(gz_n)
+    ]
+    w2_in = bring(w2_hbm, w2_v)
+    edge_in = [
+        bring(edge_hbm.at[:, own(gz * PARTS + b, part)], edges.at[b, own(gz), :]) for b in range(PARTS)
+    ]
+    mesh_in = bring(mesh_hbm, mesh_full.at[own(gz), :])
+    mown_in = bring(mesh_hbm, mesh_own)
+    eown_in = bring(edge_hbm, e_own)
+    ew1_in = bring(ew1_hbm, ew1_v)
+    ew2_in = bring(ew2_hbm, ew2_v)
+
     for copy in index_in:
         copy.wait()
     sender = send_ref[:, own(gz, mine)]
@@ -373,12 +373,14 @@
     gain_m = wide(cols[2, own(gz), :], nodes // 128)
     known = edge_sum + wide(cols[3, own(gz), :], nodes // 128) * degree
     mown_in.wait()
+    spare = stops[PARTS + 1] + 1
+    embed(stops[PARTS + 1], spare)
     for copy in relays:
         copy.wait()
     tb[4] = (sums(after, 0) + tr[0].astype(F32)).astype(BF16)
     tb[5] = (sums(before, 1) + tr[1].astype(F32)).astype(BF16)
     sum_moves += [send(tb.at[4], tr.at[4], {"gz": after}), send(tb.at[5], tr.at[5], {"gz": before})]
-    embed(stops[PARTS + 1], stops[PARTS + 2])
+    embed(spare, stops[PARTS + 2])
     settle(tiles // 2 - 1)
     for copy in sum_moves:
         copy.wait()

time: 43.4 us -> 42.6 us (0.982)
  Pallas kernels: 41.8 us -> 40.9 us
    pallas_call x1, Pallas kernels: 40.4 us -> 39.5 us  [on_device(): pl.pallas_call(functools.partial(kernel, sizes), out_shape=(pltpu.VMEM((s...]
where the time goes in v4:
time: 42.6 us; the launch traced here: 42.1 us
  Pallas kernels  40.9 us (96%)
  between operations  1.29 us (3%)
    pallas_call x1, Pallas kernels, on_device(): pl.pallas_call(functools.partial(kernel, sizes), out_shape=(pltpu.VMEM((s...  39.5 us
    pallas_call x1, Pallas kernels, on_device(): pl.pallas_call(deliver, out_shape=(jax.ShapeDtypeStruct((share, nodes), B...  1.4 us

profile of v4, /device:TPU:4, one launch (start us, length us, event | category | flops | bytes accessed | tf_op | source)
XLA Modules:
  0.0 42.1 jit_solution(4971443448447888351)
XLA Ops:
  1.3 39.5 %shard_map.158 = (bf16[128,256]{1,0:T(8,128)(2,1)S(1)}, bf16[8,128,8,128]{3,2,1,0:T(8,128)(2,1)S(1)}) custom-call(bf16[186,64,128]{2,1,0:T(8,128)(2,1)} %x_hbm.1, bf16[186,512]{1,0:T(8,128)(2,1)} %bitcast.12, bf16[512,512]{1,0:T(8,128)(2,1)} %w2_hbm.1, bf16[512,1536]{1,0:T(8,128)(2,1)} %ew1_hbm.1, bf16[512,512]{1,0:T(8,128)(2,1)} %ew2_hbm.1, ...), custom_call_target="tpu_custom_call" | custom-call | tf_op jit(solution)/shard_map/pallas_call | solution.py:425
  40.7 1.4 %shard_map.159 = (bf16[128,256]{1,0:T(8,128)(2,1)}, bf16[128,64,128]{2,1,0:T(8,128)(2,1)}) custom-call(bf16[128,256]{1,0:T(8,128)(2,1)S(1)} %get-tuple-element.6.mesh_ref, bf16[8,128,8,128]{3,2,1,0:T(8,128)(2,1)S(1)} %get-tuple-element.7.blocks_ref), custom_call_target="tpu_custom_call" | custom-call | tf_op jit(solution)/shard_map/pallas_call | solution.py:483

commit v5 on v4

--- a/solution.py
+++ b/solution.py
@@ -312,15 +312,16 @@
     acc = gath[...]
     wing = HALO * lon_cols
     acc = acc + dot(xh[0], onehot(base_n, wing)) + dot(xh[1], onehot(base_s, wing))
-    for i in range(blocks):
-        acc = acc + dot(west[i], onehot(base_w + i * 128, 128)) + dot(east[i], onehot(base_e + i * 128, 128))
+    for ref, base in ((west, base_w), (east, base_e)):
+        whole = jnp.concatenate([ref[i] for i in range(blocks)], axis=1)
+        acc = acc + dot(whole, onehot(base, blocks * 128))
     gath[...] = acc
     embed(stops[0], stops[1])
     for copy in corner_moves:
         copy.wait()
     acc = gath[...]
-    for i in range(4):
-        acc = acc + dot(corner[i], onehot(base_c + i * 128, 128))
+    whole = jnp.concatenate([corner[i] for i in range(4)], axis=1)
+    acc = acc + dot(whole, onehot(base_c, 4 * 128))
     picked = acc.astype(BF16)
 
     w2_in.wait()

time: 42.6 us -> 42.5 us (level)
  no operation moved by 1% of the time
where the time goes in v5:
time: 42.5 us; the launch traced here: 42.1 us
  Pallas kernels  40.8 us (96%)
  between operations  1.29 us (3%)
    pallas_call x1, Pallas kernels, on_device(): pl.pallas_call(functools.partial(kernel, sizes), out_shape=(pltpu.VMEM((s...  39.4 us
    pallas_call x1, Pallas kernels, on_device(): pl.pallas_call(deliver, out_shape=(jax.ShapeDtypeStruct((share, nodes), B...  1.4 us

profile of v5, /device:TPU:4, one launch (start us, length us, event | category | flops | bytes accessed | tf_op | source)
XLA Modules:
  0.0 42.1 jit_solution(18147299642784819371)
XLA Ops:
  1.3 39.4 %shard_map.158 = (bf16[128,256]{1,0:T(8,128)(2,1)S(1)}, bf16[8,128,8,128]{3,2,1,0:T(8,128)(2,1)S(1)}) custom-call(bf16[186,64,128]{2,1,0:T(8,128)(2,1)} %x_hbm.1, bf16[186,512]{1,0:T(8,128)(2,1)} %bitcast.12, bf16[512,512]{1,0:T(8,128)(2,1)} %w2_hbm.1, bf16[512,1536]{1,0:T(8,128)(2,1)} %ew1_hbm.1, bf16[512,512]{1,0:T(8,128)(2,1)} %ew2_hbm.1, ...), custom_call_target="tpu_custom_call" | custom-call | tf_op jit(solution)/shard_map/pallas_call | solution.py:426
  40.7 1.4 %shard_map.159 = (bf16[128,256]{1,0:T(8,128)(2,1)}, bf16[128,64,128]{2,1,0:T(8,128)(2,1)}) custom-call(bf16[128,256]{1,0:T(8,128)(2,1)S(1)} %get-tuple-element.6.mesh_ref, bf16[8,128,8,128]{3,2,1,0:T(8,128)(2,1)S(1)} %get-tuple-element.7.blocks_ref), custom_call_target="tpu_custom_call" | custom-call | tf_op jit(solution)/shard_map/pallas_call | solution.py:484
